TPU v7x, 32 devices: a whole 2x2x4 slice. The times are simulated.
32 devices in a mesh: batch: 4 (over y, core), tm: 2 (over x), space: 4 (over z).
Axes of the slice: x: 2, y: 2, z: 4, core: 2. Of those that a mesh axis runs over, the one named last changes fastest.
Arguments:
- clip_tokens: bfloat16 [4, 4, 32, 32, 1024], P('batch', None, 'space', 'tm'), may hold values from -6 to 6
- frame_order: int32 [4, 4], P('batch'), may hold values from 0 to 3, each once within a row
- row_reach: int32 [4, 4], P('batch', 'tm'), may hold values from 1 to 4
- spatial_gain: float32 [1024], replicated, may hold values from 0.1 to 1.9
- spatial_heads: bfloat16 [1024, 3072], replicated, may hold values from -2 to 2
- spatial_merge: bfloat16 [1024, 1024], replicated, may hold values from -0.1875 to 0.1875
- temporal_gain: float32 [1024], replicated, may hold values from 0.1 to 1.9
- temporal_heads: bfloat16 [1024, 3072], replicated, may hold values from -2 to 2
- temporal_merge: bfloat16 [1024, 1024], replicated, may hold values from -0.1875 to 0.1875
- cotangent: bfloat16 [4, 4, 32, 32, 1024], P('batch', 'tm', 'space'), may hold values from -0.059814453 to 0.059814453
Outputs:
- output: bfloat16 [4, 4, 32, 32, 1024], P('batch', 'tm', 'space')
- weight_grad: float32 [1024, 1024], P(('tm', 'space'))
Inputs may be any that keep to these rules, and one draw needn't show every extreme that they name: Each row of frame_order names every number from 0 to 3 once.
All inputs are finite; a program needn't handle non-finite values.
Results may differ from a plain program's by a relative error of at most 0.025.
Values may be sent and summed in bfloat16 or wider, within the bound.
A program may use at most 128 MiB of HBM per device.

v0:
```python
import jax
import jax.numpy as jnp
from jax import lax
from jax.sharding import PartitionSpec as P

HALO = 4
D = 1024
HEADS = 16
HEAD_DIM = 64


floor_term = 0.5


def extended(value, sides, width):
    for axis, dim in sides:
        devices, length = (lax.axis_size(axis), value.shape[dim])
        up = [(i, (i + 1) % devices) for i in range(devices - 1)]
        down = [(j, i) for i, j in up]
        last = lax.slice_in_dim(value, length - width, length, axis=dim)
        initial = lax.slice_in_dim(value, 0, width, axis=dim)
        before = lax.ppermute(last, axis, up)
        after = lax.ppermute(initial, axis, down)
        value = jnp.concatenate([before, value, after], axis=dim)
    return value


def normalize(values, gain_vector):
    widened = values.astype(jnp.float32)
    scaled = widened * lax.rsqrt(jnp.mean(widened * widened, axis=-1, keepdims=True) + floor_term)
    return (scaled * gain_vector).astype(jnp.bfloat16)


def softmax_rounded(scores, allowed):
    masked = jnp.where(allowed, scores, -1e30)
    top_score = jnp.max(masked, axis=-1, keepdims=True)
    exponent = jnp.exp(masked - top_score)
    return (exponent / jnp.sum(exponent, axis=-1, keepdims=True)).astype(jnp.bfloat16)


def temporal_attend(queries, keys_all, values_all, query_order, key_order):
    clip_count, query_frames, positions, _ = queries.shape
    key_frames = keys_all.shape[1]
    query_heads = queries.reshape(clip_count, query_frames, positions, HEADS, HEAD_DIM)
    key_heads = keys_all.reshape(clip_count, key_frames, positions, HEADS, HEAD_DIM)
    value_heads = values_all.reshape(clip_count, key_frames, positions, HEADS, HEAD_DIM)
    scores = jnp.einsum(
        "cfthd,cgthd->cthfg", query_heads, key_heads, preferred_element_type=jnp.float32
    ) * HEAD_DIM ** (-0.5)
    allowed = key_order[:, None, :] <= query_order[:, :, None]
    weights = softmax_rounded(scores, allowed[:, None, None])
    context = jnp.einsum(
        "cthfg,cgthd->cfthd", weights, value_heads, preferred_element_type=jnp.float32
    )
    return context.reshape(clip_count, query_frames, positions, D).astype(jnp.bfloat16)


def per_device(
    clip_tokens,
    frame_order,
    row_reach,
    spatial_gain,
    spatial_heads,
    spatial_merge,
    temporal_gain,
    temporal_heads,
    temporal_merge,
    cotangent,
):
    frames_here = lax.all_to_all(clip_tokens, "tm", split_axis=1, concat_axis=3, tiled=True)
    clip_count, frame_count, row_count, col_count, _ = frames_here.shape
    tokens = row_count * col_count
    normed = normalize(frames_here, spatial_gain)
    projected = jnp.dot(normed, spatial_heads, preferred_element_type=jnp.float32).astype(
        jnp.bfloat16
    )
    key_value = extended(projected[..., D:], (("space", 2),), HALO)
    extent = (row_count + 2 * HALO) * col_count
    first_row = lax.axis_index("space") * row_count
    all_rows = row_count * lax.axis_size("space")
    query_rows = first_row + jnp.arange(tokens, dtype=jnp.int32) // col_count
    key_rows = first_row - HALO + jnp.arange(extent, dtype=jnp.int32) // col_count
    inside = (key_rows >= 0) & (key_rows < all_rows)
    distance = jnp.abs(key_rows[None, :] - query_rows[:, None])

    def spatial_item(inputs):
        queries, key_pairs, reach_now = inputs
        query_heads = queries.reshape(tokens, HEADS, HEAD_DIM)
        key_heads = key_pairs[:, :D].reshape(extent, HEADS, HEAD_DIM)
        value_heads = key_pairs[:, D:].reshape(extent, HEADS, HEAD_DIM)
        scores = jnp.einsum(
            "qhd,khd->hqk", query_heads, key_heads, preferred_element_type=jnp.float32
        ) * HEAD_DIM ** (-0.5)
        allowed = inside[None, :] & (distance <= reach_now)
        weights = softmax_rounded(scores, allowed[None])
        context = jnp.einsum(
            "hqk,khd->qhd", weights, value_heads, preferred_element_type=jnp.float32
        )
        return context.reshape(tokens, D).astype(jnp.bfloat16)

    item_count = clip_count * frame_count
    spatial_context = lax.map(
        spatial_item,
        (
            projected[..., :D].reshape(item_count, tokens, D),
            key_value.reshape(item_count, extent, 2 * D),
            row_reach.reshape(item_count),
        ),
    )
    flat_input = frames_here.reshape(clip_count, frame_count, tokens, D)
    spatial_context = spatial_context.reshape(clip_count, frame_count, tokens, D)
    middle = (
        flat_input.astype(jnp.float32)
        + jnp.dot(spatial_context, spatial_merge, preferred_element_type=jnp.float32)
    ).astype(jnp.bfloat16)
    normed_two = normalize(middle, temporal_gain)
    projected_two = jnp.dot(normed_two, temporal_heads, preferred_element_type=jnp.float32).astype(
        jnp.bfloat16
    )
    regrouped = lax.all_to_all(projected_two, "tm", split_axis=2, concat_axis=1, tiled=True)
    context_all = temporal_attend(
        regrouped[..., :D],
        regrouped[..., D : 2 * D],
        regrouped[..., 2 * D :],
        frame_order,
        frame_order,
    )
    temporal_context = lax.all_to_all(context_all, "tm", split_axis=1, concat_axis=2, tiled=True)
    output = (
        middle.astype(jnp.float32)
        + jnp.dot(temporal_context, temporal_merge, preferred_element_type=jnp.float32)
    ).astype(jnp.bfloat16)
    flat_context = temporal_context.reshape(-1, D)
    flat_cotangent = cotangent.reshape(-1, D)
    own_rows = lax.psum_scatter(
        lax.dot_general(
            flat_context,
            flat_cotangent,
            (((0,), (0,)), ((), ())),
            preferred_element_type=jnp.float32,
        ).astype(jnp.bfloat16),
        ("tm", "space"),
        scatter_dimension=0,
        tiled=True,
    )
    weight_grad = lax.psum(own_rows, "batch").astype(jnp.float32)
    return (output.reshape(clip_count, frame_count, row_count, col_count, D), weight_grad)


def solution(mesh):
    in_specs = (
        P("batch", None, "space", "tm", None),
        P("batch", None),
        P("batch", "tm"),
        P(),
        P(),
        P(),
        P(),
        P(),
        P(),
        P("batch", "tm", "space", None, None),
    )
    out_specs = (P("batch", "tm", "space", None, None), P(("tm", "space"), None))
    return jax.shard_map(
        per_device, mesh=mesh, in_specs=in_specs, out_specs=out_specs, check_vma=False
    )
```

profile of v0, /device:TPU:0, one launch (start us, length us, event | category | flops | bytes accessed | tf_op | source)
XLA Modules:
  0.0 350.0 jit_solution(2444274592889547098)
XLA Ops:
  7.2 18.8 %all_to_all.42 = bf16[1,4,8,16,1024]{4,3,2,0,1:T(8,128)(2,1)S(1)} all-to-all(bf16[1,4,8,16,1024]{4,3,2,0,1:T(8,128)(2,1)} %bitcast.124), channel_id=1, replica_groups=mesh['batch'=4,'tm'=2,'space'=4] {'tm'}, dimensions={1} | all-to-all | bytes 2097152 | tf_op jit(solution)/shard_map/all_to_all | solution.py:70
  26.0 1.6 copy.90
  27.6 0.3 multiply_reduce_fusion
  28.0 6.9 %fusion.30 = bf16[1,2,8,32,3072]{4,3,2,1,0:T(8,128)(2,1)S(1)} fusion(bf16[1024,3072]{1,0:T(8,128)(2,1)} %param.16, f32[2,8,32,1024]{3,2,1,0:T(8,128)} %bitcast.122, f32[1024]{0:T(1024)S(1)} %copy-done.8, f32[2,8,32]{2,1,0:T(8,128)S(1)} %rsqrt.20), kind=kOutput, calls=%fused_computation.36 | convolution fusion | flops 3224371200 | bytes 11540480 | tf_op jit(solution)/shard_map/dot_general | solution.py:74
  34.9 1.4 fusion.63
  36.3 0.5 copy-done.3
  36.8 4.7 %collective-permute-start = (bf16[1,2,4,32,2048]{4,3,2,1,0:T(8,128)(2,1)}, bf16[1,2,4,32,2048]{4,3,2,1,0:T(8,128)(2,1)}, u32[]{:S(2)}, u32[]{:S(2)}) collective-permute-start(bf16[1,2,4,32,2048]{4,3,2,1,0:T(8,128)(2,1)} %get-tuple-element.133), channel_id=1, source_target_pairs={{0,1},{1,2},{2,3},{4,5},{5,6},{6,7},{8,9},{9,10},{10,11},{12,13},{... | collective-permute-start | bytes 3145736 | tf_op jit(solution)/shard_map/ppermute | solution.py:22
  41.5 1.5 collective-permute-start.1
  43.0 1.9 copy-done.4
  44.9 1.1 slice.43
  46.0 16.4 %collective-permute-done = bf16[1,2,4,32,2048]{4,3,2,1,0:T(8,128)(2,1)} collective-permute-done((bf16[1,2,4,32,2048]{4,3,2,1,0:T(8,128)(2,1)}, bf16[1,2,4,32,2048]{4,3,2,1,0:T(8,128)(2,1)}, u32[]{:S(2)}, u32[]{:S(2)}) %collective-permute-start) | collective-permute-done | bytes 1048608 | tf_op jit(solution)/shard_map/ppermute | solution.py:22
  62.4 4.9 %collective-permute-done.1 = bf16[1,2,4,32,2048]{4,3,2,1,0:T(8,128)(2,1)} collective-permute-done((bf16[1,2,4,32,2048]{4,3,2,1,0:T(8,128)(2,1)S(1)}, bf16[1,2,4,32,2048]{4,3,2,1,0:T(8,128)(2,1)}, u32[]{:S(2)}, u32[]{:S(2)}) %collective-permute-start.1) | collective-permute-done | bytes 1048608 | tf_op jit(solution)/shard_map/ppermute | solution.py:23
  67.3 3.4 pad_maximum_fusion
  70.7 52.0 %while.11 = (s32[]{:T(128)}, bf16[2,256,1024]{1,2,0:T(8,128)(2,1)}, bf16[2,512,2048]{2,1,0:T(8,128)(2,1)}, s32[2]{0:T(128)S(1)}, bf16[2,256,1024]{2,1,0:T(8,128)...) while((s32[]{:T(128)}, bf16[2,256,1024]{1,2,0:T(8,128)(2,1)}, ...), condition=%wide.region_4.5_spmd.clone, body=%wide.region_1.4_spmd.clone.sunk | while | flops 550246912 | bytes 44339888 | solution.py:102
  70.7 0.6 dynamic_slice.22
  71.3 0.9 fusion.89
  72.1 3.2 constant_dynamic-slice_fusion.4
  75.3 3.9 %copy.117 = bf16[1,512,2048]{1,2,0:T(8,128)(2,1)} copy(bf16[1,512,2048]{2,1,0:T(8,128)(2,1)} %constant_dynamic-slice_fusion.4) | data formatting | bytes 4194304 | tf_op jit(solution)/shard_map/while/body/jit(dynamic_index_in_dim)/dynamic_slice | solution.py:102
  79.2 3.1 fusion.88
  82.3 1.0 copy.118
  83.3 7.7 %fusion.90 = (f32[16,256]{1,0:T(8,128)S(1)}, f32[16,256,512]{2,1,0:T(8,128)}) fusion(pred[256,512]{1,0:T(8,128)(4,1)S(1)} %fusion.89, bf16[256,16,64]{0,2,1:T(8,128)(2,1)} %bitcast.111, bf16[512,16,64]{0,2,1:T(8,128)(2,1)} %bitcast.110), kind=kOutput, calls=%fused_computation.80.clone.1 | convolution fusion | flops 276824576 | bytes 10108928 | tf_op jit(solution)/shard_map/while/body/eval_jaxpr/sub | solution.py:37
  91.0 4.9 %fusion.91 = bf16[16,64,256]{2,1,0:T(8,128)(2,1)S(1)} fusion(bf16[512,16,64]{0,2,1:T(8,128)(2,1)S(1)} %bitcast.109, f32[16,256,512]{2,1,0:T(8,128)} %get-tuple-element.192, f32[16,256]{1,0:T(8,128)S(1)} %get-tuple-element.193), kind=kOutput, calls=%fused_computation.11.clone.1 | convolution fusion | flops 272891904 | bytes 9977856 | tf_op jit(solution)/shard_map/while/body/eval_jaxpr/hqk,khd->qhd/dot_general | solution.py:96
  95.8 0.8 constant_dynamic-update-slice_fusion.2
  96.7 0.6 dynamic_slice.22
  97.2 0.9 fusion.89
  98.1 3.2 constant_dynamic-slice_fusion.4
  101.3 3.9 %copy.117 = bf16[1,512,2048]{1,2,0:T(8,128)(2,1)} copy(bf16[1,512,2048]{2,1,0:T(8,128)(2,1)} %constant_dynamic-slice_fusion.4) | data formatting | bytes 4194304 | tf_op jit(solution)/shard_map/while/body/jit(dynamic_index_in_dim)/dynamic_slice | solution.py:102
  105.2 3.1 fusion.88
  108.3 1.0 copy.118
  109.3 7.6 %fusion.90 = (f32[16,256]{1,0:T(8,128)S(1)}, f32[16,256,512]{2,1,0:T(8,128)}) fusion(pred[256,512]{1,0:T(8,128)(4,1)S(1)} %fusion.89, bf16[256,16,64]{0,2,1:T(8,128)(2,1)} %bitcast.111, bf16[512,16,64]{0,2,1:T(8,128)(2,1)} %bitcast.110), kind=kOutput, calls=%fused_computation.80.clone.1 | convolution fusion | flops 276824576 | bytes 10108928 | tf_op jit(solution)/shard_map/while/body/eval_jaxpr/sub | solution.py:37
  116.9 4.9 %fusion.91 = bf16[16,64,256]{2,1,0:T(8,128)(2,1)S(1)} fusion(bf16[512,16,64]{0,2,1:T(8,128)(2,1)S(1)} %bitcast.109, f32[16,256,512]{2,1,0:T(8,128)} %get-tuple-element.192, f32[16,256]{1,0:T(8,128)S(1)} %get-tuple-element.193), kind=kOutput, calls=%fused_computation.11.clone.1 | convolution fusion | flops 272891904 | bytes 9977856 | tf_op jit(solution)/shard_map/while/body/eval_jaxpr/hqk,khd->qhd/dot_general | solution.py:96
  121.8 0.8 constant_dynamic-update-slice_fusion.2
  122.6 3.3 fusion.36
  125.9 1.0 copy-done.12
  126.9 6.6 %fusion.33 = bf16[1,2,256,3072]{3,2,1,0:T(8,128)(2,1)S(1)} fusion(bf16[1024,3072]{1,0:T(8,128)(2,1)} %param.19, bf16[2,256,1024]{2,1,0:T(8,128)(2,1)S(1)} %get-tuple-element.136, f32[1024]{0:T(1024)S(1)} %copy-done.9, f32[2,256]{1,0:T(2,128)S(1)} %add_rsqrt_fusion.1), kind=kOutput, calls=%fused_computation.37 | convolution fusion | flops 3224895488 | bytes 10491904 | tf_op jit(solution)/shard_map/dot_general | solution.py:117
  133.5 4.9 %copy.95 = bf16[1,2,256,3072]{3,1,0,2:T(2,128)(2,1)} copy(bf16[1,2,256,3072]{3,2,1,0:T(8,128)(2,1)S(1)} %fusion.33) | data formatting | bytes 6291456 | tf_op jit(solution)/shard_map/convert_element_type | solution.py:117
  138.4 5.3 %all-to-all-start.1 = ((bf16[1,2,256,3072]{3,1,0,2:T(2,128)(2,1)}), bf16[1,2,256,3072]{3,1,0,2:T(2,128)(2,1)}, u32[]{:S(2)}, u32[]{:S(2)}) async-start(bf16[1,2,256,3072]{3,1,0,2:T(2,128)(2,1)} %copy.95), calls=%async_computation.1 | async-start | bytes 6291456 | tf_op jit(solution)/shard_map/all_to_all | solution.py:120
  143.7 0.3 reduce-scatter.2.cloned.1.call-start
  144.1 34.1 %all-to-all-done.1 = bf16[1,2,256,3072]{3,1,0,2:T(2,128)(2,1)} async-done(((bf16[1,2,256,3072]{3,1,0,2:T(2,128)(2,1)}), bf16[1,2,256,3072]{3,1,0,2:T(2,128)(2,1)}, u32[]{:S(2)}, u32[]{:S(2)}) %all-to-all-start.1) | async-done | bytes 3145760 | tf_op jit(solution)/shard_map/all_to_all | solution.py:120
  178.2 2.7 copy.96
  180.8 0.2 copy.97
  181.0 1.8 fusion.62
  182.8 1.6 copy.99
  184.4 3.0 copy.101
  187.4 1.6 copy.100
  189.0 2.9 copy.102
  192.0 6.5 %fusion.64 = f32[128,16,4,4]{2,3,1,0:T(4,128)} fusion(bf16[4,128,16,64]{3,0,2,1:T(4,128)(2,1)} %copy.101, bf16[4,128,16,64]{3,0,2,1:T(4,128)(2,1)} %copy.102), kind=kOutput, calls=%fused_computation.83 | convolution fusion | flops 4194304 | bytes 2228224 | tf_op jit(solution)/shard_map/cfthd,cgthd->cthfg/dot_general | solution.py:47
  198.5 3.8 %copy.103 = f32[128,16,4,4]{0,1,3,2:T(8,128)S(1)} copy(f32[128,16,4,4]{2,3,1,0:T(4,128)} %fusion.64) | data formatting | bytes 262144 | tf_op jit(solution)/shard_map/cfthd,cgthd->cthfg/dot_general | solution.py:47
  202.3 0.1 fusion.54
  202.4 0.1 divide_convert_fusion.4
  202.5 4.3 %copy.105 = bf16[128,16,4,4]{3,2,1,0:T(4,128)(2,1)} copy(bf16[128,16,4,4]{0,1,3,2:T(8,128)(2,1)S(1)} %divide_convert_fusion.4) | data formatting | bytes 131072 | tf_op jit(solution)/shard_map/convert_element_type | solution.py:38
  206.9 1.6 copy.98
  208.5 2.9 copy.104
  211.4 5.9 %convert_bitcast_fusion = bf16[1,4,128,16,64]{4,1,3,2,0:T(4,128)(2,1)} fusion(bf16[4,128,16,64]{3,0,2,1:T(4,128)(2,1)} %copy.104, bf16[128,16,4,4]{3,2,1,0:T(4,128)(2,1)} %copy.105), kind=kOutput, calls=%fused_computation.49 | convolution fusion | flops 4718592 | bytes 2162688 | tf_op jit(solution)/shard_map/cthfg,cgthd->cfthd/dot_general | solution.py:52
  217.3 3.5 copy.106
  220.8 14.2 %all_to_all.43 = bf16[1,4,128,1024]{2,3,0,1:T(8,128)(2,1)} all-to-all(bf16[1,4,128,1024]{2,3,0,1:T(8,128)(2,1)S(1)} %bitcast.120), channel_id=1, replica_groups=mesh['batch'=4,'tm'=2,'space'=4] {'tm'}, dimensions={1} | all-to-all | bytes 2097152 | tf_op jit(solution)/shard_map/all_to_all | solution.py:128
  235.0 1.5 copy.108
  236.6 1.0 copy-done.5
  237.6 0.5 copy-done.7
  238.1 2.6 convolution_convert_fusion
  240.8 66.8 %reduce-scatter.2.cloned.1.call-done = bf16[128,1024]{1,0:T(8,128)(2,1)} async-done(((bf16[1024,1024]{1,0:T(8,128)(2,1)}), bf16[128,1024]{1,0:T(8,128)(2,1)}) %reduce-scatter.2.cloned.1.call-update) | async-done | bytes 262160 | tf_op jit(solution)/shard_map/reduce_scatter | solution.py:135
  307.7 4.1 %fusion.39 = bf16[2,256,1024]{2,1,0:T(8,128)(2,1)} fusion(bf16[2,256,1024]{2,1,0:T(8,128)(2,1)} %copy-done.12, bf16[2,256,1024]{2,1,0:T(8,128)(2,1)S(1)} %bitcast.126, bf16[1024,1024]{1,0:T(8,128)(2,1)} %param.20), kind=kOutput, calls=%fused_computation.44 | convolution fusion | flops 1075314688 | bytes 5242880 | tf_op jit(solution)/shard_map/dot_general | solution.py:131
  311.7 29.6 %all-reduce.2.cloned.1.call-done = bf16[128,1024]{1,0:T(8,128)(2,1)} async-done(((bf16[128,1024]{1,0:T(8,128)(2,1)}), bf16[128,1024]{1,0:T(8,128)(2,1)}) %all-reduce.2.cloned.1.call-update) | async-done | bytes 262160 | tf_op jit(solution)/shard_map/psum | solution.py:146
  341.4 1.8 convert_element_type.136
  (44 shorter events, 0.6 us)
Async XLA Ops:
  7.2 115.5 %copy-start = (bf16[1024,1024]{1,0:T(8,128)(2,1)S(1)}, bf16[1024,1024]{1,0:T(8,128)(2,1)}, u32[]{:S(2)}) copy-start(bf16[1024,1024]{1,0:T(8,128)(2,1)} %param.17) | copy-start | bytes 6291460
  26.0 2.0 copy-start.8
  34.9 1.9 copy-start.3
  36.8 25.6 %collective-permute-start = (bf16[1,2,4,32,2048]{4,3,2,1,0:T(8,128)(2,1)}, bf16[1,2,4,32,2048]{4,3,2,1,0:T(8,128)(2,1)}, u32[]{:S(2)}, u32[]{:S(2)}) collective-permute-start(bf16[1,2,4,32,2048]{4,3,2,1,0:T(8,128)(2,1)} %get-tuple-element.133), channel_id=1, source_target_pairs={{0,1},{1,2},{2,3},{4,5},{5,6},{6,7},{8,9},{9,10},{10,11},{12,13},{... | collective-permute-start | bytes 3145736 | tf_op jit(solution)/shard_map/ppermute | solution.py:22
  41.5 25.8 %collective-permute-start.1 = (bf16[1,2,4,32,2048]{4,3,2,1,0:T(8,128)(2,1)S(1)}, bf16[1,2,4,32,2048]{4,3,2,1,0:T(8,128)(2,1)}, u32[]{:S(2)}, u32[]{:S(2)}) collective-permute-start(bf16[1,2,4,32,2048]{4,3,2,1,0:T(8,128)(2,1)S(1)} %get-tuple-element.134), channel_id=1, source_target_pairs={{1,0},{2,1},{3,2},{5,4},{6,5},{7,6},{9,8},{10,9},{11,10},{13,12},{... | collective-permute-start | bytes 3145736 | tf_op jit(solution)/shard_map/ppermute | solution.py:23
  43.0 1.9 copy-start.4
  44.9 22.3 %slice-start = ((bf16[1,2,8,32,3072]{4,3,2,1,0:T(8,128)(2,1)}), bf16[1,2,8,32,2048]{4,3,2,1,0:T(8,128)(2,1)S(1)}, s32[]{:S(2)}) async-start(bf16[1,2,8,32,3072]{4,3,2,1,0:T(8,128)(2,1)} %copy-done.3), calls=%async_computation.6 | async-start | bytes 4194304 | tf_op jit(solution)/shard_map/slice | solution.py:77
  46.0 24.7 %copy-start.10 = (s32[1,2]{1,0:T(1,128)S(1)}, s32[1,2]{1,0:T(1,128)}, u32[]{:S(2)}) copy-start(s32[1,2]{1,0:T(1,128)} %param.14) | copy-start | bytes 28
  79.2 3.1 copy-start.2
  83.3 7.7 %copy-start.1 = (bf16[512,1024]{0,1:T(8,128)(2,1)S(1)}, bf16[512,1024]{0,1:T(8,128)(2,1)}, u32[]{:S(2)}) copy-start(bf16[512,1024]{0,1:T(8,128)(2,1)} %get-tuple-element.190) | copy-start | bytes 3145732 | tf_op jit(solution)/shard_map/while
  105.2 3.1 copy-start.2
  109.3 7.6 %copy-start.1 = (bf16[512,1024]{0,1:T(8,128)(2,1)S(1)}, bf16[512,1024]{0,1:T(8,128)(2,1)}, u32[]{:S(2)}) copy-start(bf16[512,1024]{0,1:T(8,128)(2,1)} %get-tuple-element.190) | copy-start | bytes 3145732 | tf_op jit(solution)/shard_map/while
  122.6 4.3 %copy-start.9 = (f32[1024]{0:T(1024)S(1)}, f32[1024]{0:T(1024)}, u32[]{:S(2)}) copy-start(f32[1024]{0:T(1024)} %param.18) | copy-start | bytes 12292
  125.9 1.0 copy-start.12
  138.4 5.6 %copy-start.11 = (s32[1,4]{1,0:T(1,128)S(1)}, s32[1,4]{1,0:T(1,128)}, u32[]{:S(2)}) copy-start(s32[1,4]{1,0:T(1,128)} %param.13) | copy-start | bytes 52
  138.4 39.8 %all-to-all-start.1 = ((bf16[1,2,256,3072]{3,1,0,2:T(2,128)(2,1)}), bf16[1,2,256,3072]{3,1,0,2:T(2,128)(2,1)}, u32[]{:S(2)}, u32[]{:S(2)}) async-start(bf16[1,2,256,3072]{3,1,0,2:T(2,128)(2,1)} %copy.95), calls=%async_computation.1 | async-start | bytes 6291456 | tf_op jit(solution)/shard_map/all_to_all | solution.py:120
  143.7 163.9 %reduce-scatter.2.cloned.1.call-start = ((), (), s32[]{:S(2)}) async-start(), calls=%async_computation.4 | async-start | bytes 2359296 | tf_op jit(solution)/shard_map/reduce_scatter | solution.py:135
  236.5 1.6 copy-start.7
  236.6 1.0 copy-start.5
  240.7 66.9 %copy-start.6 = (bf16[1,2,2,128,1024]{4,3,2,1,0:T(8,128)(2,1)S(1)}, bf16[1,2,2,128,1024]{4,3,2,1,0:T(8,128)(2,1)}, u32[]{:S(2)}) copy-start(bf16[1,2,2,128,1024]{4,3,2,1,0:T(8,128)(2,1)} %copy-done.5) | copy-start | bytes 3145732
  240.8 100.6 %all-reduce.2.cloned.1.call-start = ((), (), s32[]{:S(2)}) async-start(), calls=%async_computation.5 | async-start | bytes 524288 | tf_op jit(solution)/shard_map/psum | solution.py:146
Sparse Core Ops, SparseCore 0:
  240.9 66.6 reduce-scatter.1
  309.9 31.3 all-reduce.1
where the time goes:
time: 351 us; the launch traced here: 350 us
  waiting for transfers between devices  152 us (43%)
  local copies, waits for them, and re-layouts  70.6 us (20%)
  matrix products  60.8 us (17%)
  blocking collectives  33 us (9%)
  between operations  14.3 us (4%)
  starting transfers between devices  11.8 us (3%)
  other arithmetic  7.61 us (2%)
    reduce_scatter x1, waiting for transfers between devices, per_device(): lax.psum_scatter(lax.dot_general(flat_context, flat_cotangent, (((0,), (0...  66.8 us
    all_to_all x1, waiting for transfers between devices, per_device(): lax.all_to_all(projected_two, 'tm', split_axis=2, concat_axis=1, tiled=True)  34.1 us
    psum x1, waiting for transfers between devices, per_device(): weight_grad = lax.psum(own_rows, 'batch').astype(jnp.float32)  29.6 us
    all_to_all x1, blocking collectives, per_device(): lax.all_to_all(clip_tokens, 'tm', split_axis=1, concat_axis=3, tiled=True)  18.8 us
    dynamic_slice x10, local copies, waits for them, and re-layouts, per_device(): lax.map(spatial_item, (projected[..., :D].reshape(item_count, tokens, D),...  17.4 us
    ppermute x1, waiting for transfers between devices, extended(): before = lax.ppermute(last, axis, up)  16.4 us
    sub x2, matrix products, softmax_rounded(): exponent = jnp.exp(masked - top_score)  15.3 us
    all_to_all x1, blocking collectives, per_device(): lax.all_to_all(context_all, 'tm', split_axis=1, concat_axis=2, tiled=True)  14.2 us
  transfers between devices with their start and end apart: 5, of which 5 were waited for; matrix products, arithmetic and copies ran while one was open for 2% of the time, Pallas kernels for 0%

commit v1 on v0

v1 whole, which is shorter than its diff:
```python
import functools

import jax
import jax.numpy as jnp
from jax import lax
from jax.experimental import pallas as pl
from jax.experimental.pallas import tpu as pltpu
from jax.sharding import PartitionSpec as P

HALO = 4
HEADS = 16
HEAD_DIM = 64
LANES = 128
SCALE = HEAD_DIM ** (-0.5)
FLOOR = 0.5
BF = jnp.bfloat16
F32 = jnp.float32


def normalize(values, gain_vector):
    widened = values.astype(F32)
    scaled = widened * lax.rsqrt(jnp.mean(widened * widened, axis=-1, keepdims=True) + FLOOR)
    return (scaled * gain_vector).astype(BF)


def spatial_kernel(rows, cols, all_rows, reach_ref, first_ref, q_ref, k_ref, v_ref, kt_ref, vt_ref,
                   kb_ref, vb_ref, o_ref, kx, vx, bias):
    frame, block = pl.program_id(0), pl.program_id(1)
    span = HALO * cols
    window = 3 * span
    chunks = rows // HALO

    @pl.when(block == 0)
    def _():
        reach, first = reach_ref[frame], first_ref[0]
        for chunk in range(chunks):
            shape = (span, window)
            q_row = chunk * HALO + lax.broadcasted_iota(jnp.int32, shape, 0) // cols
            k_row = (chunk - 1) * HALO + lax.broadcasted_iota(jnp.int32, shape, 1) // cols
            place = first + k_row
            kept = (jnp.abs(k_row - q_row) <= reach) & (place >= 0) & (place < all_rows)
            bias[chunk] = jnp.where(kept, 0.0, -1e30)

    tokens = rows * cols
    for own, top, low, joined in ((k_ref, kt_ref, kb_ref, kx), (v_ref, vt_ref, vb_ref, vx)):
        joined[:span] = top[...]
        joined[span:span + tokens] = own[...]
        joined[span + tokens:] = low[...]

    lane = lax.broadcasted_iota(jnp.int32, (1, LANES), 1)
    first_head = (lane < HEAD_DIM).astype(F32)
    masks = (first_head.astype(BF), (1.0 - first_head).astype(BF))
    for pair in range(q_ref.shape[1] // LANES):
        at = slice(pair * LANES, (pair + 1) * LANES)
        for chunk in range(chunks):
            here = slice(chunk * span, (chunk + 1) * span)
            near = slice(chunk * span, chunk * span + window)
            q = q_ref[here, at] * BF(SCALE)
            k = kx[near, at]
            v = vx[near, at]
            outs = []
            for head in range(2):
                s = lax.dot_general(q * masks[head], k, (((1,), (1,)), ((), ())),
                                    preferred_element_type=F32) + bias[chunk]
                top_score = jnp.max(s, axis=-1, keepdims=True)
                p = jnp.exp(s - top_score).astype(BF)
                o = jnp.dot(p, v * masks[head] + masks[1 - head], preferred_element_type=F32)
                outs.append(o / pltpu.roll(o, HEAD_DIM, 1))
            o_ref[here, at] = jnp.where(lane < HEAD_DIM, outs[0], outs[1]).astype(BF)


def spatial_attend(projected, halo, reach, first_row, frames, rows, cols, all_rows):
    depth = projected.shape[1] // 3
    tokens, span = rows * cols, HALO * cols
    width = 2 * LANES
    blocks = depth // width
    here = lambda part: pl.BlockSpec((tokens, width), lambda f, j: (f, part * blocks + j))
    beside = lambda side, part: pl.BlockSpec(
        (span, width), lambda f, j: (side * frames + f, part * blocks + j))
    smem = pl.BlockSpec(memory_space=pltpu.SMEM)
    pairs = frames * HEADS * tokens * 3 * span
    return pl.pallas_call(
        functools.partial(spatial_kernel, rows, cols, all_rows),
        grid=(frames, blocks),
        out_shape=jax.ShapeDtypeStruct((frames * tokens, depth), BF),
        in_specs=[smem, smem, here(0), here(1), here(2), beside(0, 0), beside(0, 1), beside(1, 0), beside(1, 1)],
        out_specs=pl.BlockSpec((tokens, width), lambda f, j: (f, j)),
        scratch_shapes=[
            pltpu.VMEM((tokens + 2 * span, width), BF),
            pltpu.VMEM((tokens + 2 * span, width), BF),
            pltpu.VMEM((rows // HALO, span, 3 * span), F32),
        ],
        cost_estimate=pl.CostEstimate(flops=4 * pairs * LANES, bytes_accessed=frames * tokens * depth * 12,
                                      transcendentals=pairs),
        name="spatial",
    )(reach, first_row, projected, projected, projected, halo, halo, halo, halo)


def temporal_kernel(others, q_order, k_order, gather_ref, spread_ref, q_ref, *refs):
    k_refs, v_refs, o_ref = refs[:others + 1], refs[others + 1:2 * others + 2], refs[-1]
    frames = q_ref.shape[0]
    keys = [(ref, i) for ref in k_refs for i in range(frames)]
    values = [(ref, i) for ref in v_refs for i in range(frames)]
    for f in range(frames):
        q = q_ref[f] * BF(SCALE)
        scores = []
        for g, (ref, i) in enumerate(keys):
            s = jnp.dot(q * ref[i], gather_ref[...], preferred_element_type=F32)
            scores.append(s + jnp.where(k_order[g] <= q_order[f], 0.0, -1e30))
        top_score = functools.reduce(jnp.maximum, scores)
        exps = [jnp.exp(s - top_score) for s in scores]
        scale = 1.0 / functools.reduce(jnp.add, exps)
        total = None
        for g, (ref, i) in enumerate(values):
            w = jnp.dot((exps[g] * scale).astype(BF), spread_ref[...], preferred_element_type=F32)
            term = w * ref[i].astype(F32)
            total = term if total is None else total + term
        o_ref[f] = total.astype(BF)


def temporal_attend(own, others, q_order, k_order, frames):
    depth = own.shape[1] // 3
    tokens = own.shape[0] // frames
    size = min(tokens, 64)
    head = jnp.arange(depth, dtype=jnp.int32) // HEAD_DIM
    gather = (head[:, None] == jnp.arange(LANES, dtype=jnp.int32)[None, :]).astype(BF)
    own = own.reshape(frames, tokens, 3 * depth)
    others = [value.reshape(frames, tokens, 2 * depth) for value in others]
    part = lambda column: pl.BlockSpec((frames, size, depth), lambda i: (0, i, column))
    smem = pl.BlockSpec(memory_space=pltpu.SMEM)
    whole = lambda shape: pl.BlockSpec(shape, lambda i: (0, 0))
    count = len(others)
    keys = (count + 1) * frames
    out = pl.pallas_call(
        functools.partial(temporal_kernel, count),
        grid=(tokens // size,),
        out_shape=jax.ShapeDtypeStruct((frames, tokens, depth), BF),
        in_specs=[smem, smem, whole((depth, LANES)), whole((LANES, depth)), part(0)]
        + [part(1)] + [part(0)] * count + [part(2)] + [part(1)] * count,
        out_specs=part(0),
        cost_estimate=pl.CostEstimate(flops=4 * frames * keys * tokens * depth * LANES,
                                      bytes_accessed=4 * keys * tokens * depth, transcendentals=0),
        name="temporal",
    )(q_order, k_order, gather, gather.T, own, own, *others, own, *others)
    return out.reshape(frames * tokens, depth)


def cyclic(axis, shift):
    n = lax.axis_size(axis)
    return [(i, (i + shift) % n) for i in range(n)]


def exchange_bit(value, axis, bit):
    n = lax.axis_size(axis)
    return lax.ppermute(value, axis, [(i, i ^ bit) for i in range(n)])


def halve_columns(value, bit):
    half = value.shape[1] // 2
    mine = lax.axis_index("batch") // bit % 2
    sent = lax.dynamic_slice_in_dim(value, (1 - mine) * half, half, 1)
    kept = lax.dynamic_slice_in_dim(value, mine * half, half, 1)
    arrived = exchange_bit(sent, "batch", bit)
    return (kept.astype(F32) + arrived.astype(F32)).astype(BF)


def scatter_rows(value, axis):
    n, me = lax.axis_size(axis), lax.axis_index(axis)
    size = value.shape[0] // n
    take = lambda owner: lax.dynamic_slice_in_dim(value, owner * size, size, 0)
    total = take(me).astype(F32)
    for shift in range(1, n):
        arrived = lax.ppermute(take((me + shift) % n), axis, cyclic(axis, shift))
        total = total + arrived.astype(F32)
    return total.astype(BF)


def reduce_gradient(part):
    n, me = lax.axis_size("batch"), lax.axis_index("batch")
    bits = [1 << i for i in range(n.bit_length() - 1)]
    part = halve_columns(part, bits[0])
    half = part.shape[1] // 2
    one, two = part[:, :half], part[:, half:]
    for bit in bits[1:]:
        one = halve_columns(one, bit)
    two = scatter_rows(two, "tm")
    one = scatter_rows(one, "tm")
    for bit in bits[1:]:
        two = halve_columns(two, bit)
    piece = scatter_rows(jnp.concatenate([one, two], axis=1), "space")
    pieces = [piece] + [exchange_bit(piece, "batch", d) for d in range(1, n)]
    placed = [lax.select_n(me ^ b, *pieces) for b in range(n)]
    small = piece.shape[1] // 2

    def ordered(prefix, left):
        if not left:
            return [placed[prefix]]
        return ordered(prefix, left[1:]) + ordered(prefix + left[0], left[1:])

    columns = []
    for first in (0, bits[0]):
        owners = ordered(first, bits[1:])
        columns += [owner[:, :small] for owner in owners] + [owner[:, small:] for owner in owners]
    return jnp.concatenate(columns, axis=1).astype(F32)


def per_device(clip_tokens, frame_order, row_reach, spatial_gain, spatial_heads, spatial_merge,
               temporal_gain, temporal_heads, temporal_merge, cotangent):
    ranks, me = lax.axis_size("tm"), lax.axis_index("tm")
    places, place = lax.axis_size("space"), lax.axis_index("space")
    _, all_frames, rows, part_cols, depth = clip_tokens.shape
    frames, cols = all_frames // ranks, part_cols * ranks
    tokens, span = rows * cols, HALO * cols
    clip = clip_tokens[0]
    pieces = []
    for shift in range(ranks):
        block = lax.dynamic_slice_in_dim(clip, (me + shift) % ranks * frames, frames, 0)
        pieces.append(lax.ppermute(block, "tm", cyclic("tm", shift)) if shift else block)
    here = jnp.stack([lax.select_n((me - j) % ranks, *pieces) if ranks > 2 else
                      jnp.where(me == j, pieces[0], pieces[1]) for j in range(ranks)], axis=2)
    here = here.reshape(frames, rows, cols, depth)
    up = [(i, i + 1) for i in range(places - 1)]
    down = [(i + 1, i) for i in range(places - 1)]
    above = lax.ppermute(here[:, rows - HALO:], "space", up).reshape(frames * span, depth)
    below = lax.ppermute(here[:, :HALO], "space", down).reshape(frames * span, depth)
    flat = here.reshape(frames * tokens, depth)
    projected = jnp.dot(normalize(flat, spatial_gain), spatial_heads, preferred_element_type=F32).astype(BF)
    halo = normalize(jnp.concatenate([above, below]), spatial_gain)
    halo = jnp.dot(halo, spatial_heads[:, depth:], preferred_element_type=F32).astype(BF)
    first_row = (place * rows).astype(jnp.int32).reshape(1)
    context = spatial_attend(projected, halo, row_reach.reshape(-1), first_row, frames, rows, cols, rows * places)
    middle = (flat.astype(F32) + jnp.dot(context, spatial_merge, preferred_element_type=F32)).astype(BF)

    order = frame_order.reshape(-1)
    orders = [lax.dynamic_slice_in_dim(order, (me - shift) % ranks * frames, frames, 0) for shift in range(ranks)]
    arrived = [lax.ppermute(middle, "tm", cyclic("tm", shift)) for shift in range(1, ranks)]
    own = jnp.dot(normalize(middle, temporal_gain), temporal_heads, preferred_element_type=F32).astype(BF)
    others = [jnp.dot(normalize(value, temporal_gain), temporal_heads[:, depth:],
                      preferred_element_type=F32).astype(BF) for value in arrived]
    context = temporal_attend(own, others, orders[0], jnp.concatenate(orders), frames)
    part = lax.dot_general(context, cotangent.reshape(-1, depth), (((0,), (0,)), ((), ())),
                           preferred_element_type=F32).astype(BF)
    weight_grad = reduce_gradient(part)
    output = (middle.astype(F32) + jnp.dot(context, temporal_merge, preferred_element_type=F32)).astype(BF)
    return output.reshape(1, frames, rows, cols, depth), weight_grad


def solution(mesh):
    in_specs = (
        P("batch", None, "space", "tm", None),
        P("batch", None),
        P("batch", "tm"),
        P(),
        P(),
        P(),
        P(),
        P(),
        P(),
        P("batch", "tm", "space", None, None),
    )
    out_specs = (P("batch", "tm", "space", None, None), P(("tm", "space"), None))
    return jax.shard_map(per_device, mesh=mesh, in_specs=in_specs, out_specs=out_specs, check_vma=False)
```

time: 351 us -> 146 us (0.42)
  waiting for transfers between devices: 152 us -> 41.9 us
  local copies, waits for them, and re-layouts: 70.6 us -> 6.47 us
  blocking collectives: 33 us -> 0 us
  Pallas kernels: 0 us -> 28.3 us
  matrix products: 60.8 us -> 34.1 us
  between operations: 14.3 us -> 1.01 us
  starting transfers between devices: 11.8 us -> 24.8 us
    reduce_scatter x1 -> x0, waiting for transfers between devices: 66.8 us -> none  [per_device(): lax.psum_scatter(lax.dot_general(flat_context, flat_cotangent, (((0,), (0...]
    all_to_all x1 -> x0, waiting for transfers between devices: 34.1 us -> none  [per_device(): lax.all_to_all(projected_two, 'tm', split_axis=2, concat_axis=1, tiled=True)]
    all_to_all x2 -> x0, blocking collectives: 33 us -> none  [the longest x1 18.8 us: per_device(): lax.all_to_all(clip_tokens, 'tm', split_axis=1, concat_axis=3, tiled=True)]
    psum x1 -> x0, waiting for transfers between devices: 29.6 us -> none  [per_device(): weight_grad = lax.psum(own_rows, 'batch').astype(jnp.float32)]
    pallas_call x0 -> x2, Pallas kernels: none -> 28.3 us  [the longest x1 21.3 us: spatial_attend(): pl.pallas_call(functools.partial(spatial_kernel, rows, cols, all_rows), g...]
    ppermute x2 -> x15, waiting for transfers between devices: 21.2 us -> 41.9 us  [the longest x1 13.9 us: per_device(): lax.ppermute(middle, 'tm', cyclic('tm', shift))]
    ppermute x2 -> x15, starting transfers between devices: 6.15 us -> 24.8 us  [the longest x5 8.76 us: scatter_rows(): arrived = lax.ppermute(take((me + shift) % n), axis, cyclic(axis, shift))]
    sub x2 -> x0, matrix products: 15.3 us -> none  [softmax_rounded(): exponent = jnp.exp(masked - top_score)]
  transfers between devices with their start and end apart: 5 -> 15, of which waited for: 5 -> 10; matrix products, arithmetic and copies ran while one was open for 2% -> 17% of each run, Pallas kernels for 0% -> 0%
where the time goes in v1:
time: 146 us
  waiting for transfers between devices  41.9 us (29%)
  matrix products  34.1 us (23%)
  Pallas kernels  28.3 us (19%)
  starting transfers between devices  24.8 us (17%)
  other arithmetic  9.26 us (6%)
  local copies, waits for them, and re-layouts  6.47 us (4%)
    pallas_call x1, Pallas kernels, spatial_attend(): pl.pallas_call(functools.partial(spatial_kernel, rows, cols, all_rows), g...  21.3 us
    ppermute x1, waiting for transfers between devices, per_device(): lax.ppermute(middle, 'tm', cyclic('tm', shift))  13.9 us
    ppermute x5, waiting for transfers between devices, scatter_rows(): arrived = lax.ppermute(take((me + shift) % n), axis, cyclic(axis, shift))  12.6 us
    ppermute x1, waiting for transfers between devices, per_device(): lax.ppermute(block, 'tm', cyclic('tm', shift))  8.95 us
    ppermute x5, starting transfers between devices, scatter_rows(): arrived = lax.ppermute(take((me + shift) % n), axis, cyclic(axis, shift))  8.76 us
    dot_general x1, matrix products, per_device(): jnp.dot(normalize(middle, temporal_gain), temporal_heads, preferred_eleme...  7.86 us
    dot_general x1, matrix products, per_device(): jnp.dot(normalize(flat, spatial_gain), spatial_heads, preferred_element_t...  7.73 us
    pallas_call x1, Pallas kernels, temporal_attend(): pl.pallas_call(functools.partial(temporal_kernel, count), grid=(tokens //...  7.04 us
  transfers between devices with their start and end apart: 15, of which 10 were waited for; matrix products, arithmetic and copies ran while one was open for 17% of the time, Pallas kernels for 0%

profile of v1, /device:TPU:0, one launch (start us, length us, event | category | flops | bytes accessed | tf_op | source)
XLA Modules:
  0.0 145.8 jit_solution(14192250299917701081)
XLA Ops:
  0.6 0.0 copy-start
  0.7 1.2 dynamic-slice_bitcast_fusion
  1.9 3.0 %collective-permute-start = (bf16[2,8,16,1024]{3,2,1,0:T(8,128)(2,1)S(1)}, bf16[2,8,16,1024]{3,2,1,0:T(8,128)(2,1)}, u32[]{:S(2)}, u32[]{:S(2)}) collective-permute-start(bf16[2,8,16,1024]{3,2,1,0:T(8,128)(2,1)S(1)} %dynamic-slice_bitcast_fusion), channel_id=1, source_target_pairs={{0,4},{4,0},{1,5},{5,1},{2,6},{6,2},{3,7},{7,3},{8,12},{12,8},{9,1... | collective-permute-start | bytes 1572872 | tf_op jit(solution)/shard_map/ppermute | solution.py:218
  4.9 0.8 fusion.45
  5.7 0.6 pad_add_fusion.k_order
  6.3 0.9 fusion.35.gather_ref
  7.3 0.8 fusion.36.spread_ref
  8.0 8.9 %collective-permute-done = bf16[2,8,16,1024]{3,2,1,0:T(8,128)(2,1)} collective-permute-done((bf16[2,8,16,1024]{3,2,1,0:T(8,128)(2,1)S(1)}, bf16[2,8,16,1024]{3,2,1,0:T(8,128)(2,1)}, u32[]{:S(2)}, u32[]{:S(2)}) %collective-permute-start) | collective-permute-done | bytes 524320 | tf_op jit(solution)/shard_map/ppermute | solution.py:218
  17.0 1.3 fusion.33
  18.2 0.1 pad_maximum_fusion
  18.4 0.0 copy-start.4
  18.4 0.3 fusion.20
  18.7 0.7 copy-done.1
  19.3 1.1 fusion.48
  20.4 1.3 collective-permute-start.2
  21.7 5.3 %collective-permute-start.1 = (bf16[2,4,32,1024]{3,2,1,0:T(8,128)(2,1)}, bf16[2,4,32,1024]{3,2,1,0:T(8,128)(2,1)}, u32[]{:S(2)}, u32[]{:S(2)}) collective-permute-start(bf16[2,4,32,1024]{3,2,1,0:T(8,128)(2,1)} %get-tuple-element.8), channel_id=1, source_target_pairs={{0,1},{1,2},{2,3},{4,5},{5,6},{6,7},{8,9},{9,10},{10,11},{12,13},{... | collective-permute-start | bytes 1572872 | tf_op jit(solution)/shard_map/ppermute | solution.py:224
  27.0 0.1 rsqrt.36
  27.1 0.3 fusion.22
  27.5 0.0 slice-start.1
  27.5 7.7 %convolution_convert_fusion.1.q_ref.k_ref.v_ref = bf16[512,3072]{1,0:T(8,128)(2,1)} fusion(bf16[512,1024]{1,0:T(8,128)(2,1)S(1)} %fusion.22, bf16[1024,3072]{1,0:T(8,128)(2,1)} %param.14), kind=kOutput, calls=%fused_computation.1 | convolution fusion | flops 3222798336 | bytes 10485760 | tf_op jit(solution)/shard_map/dot_general | solution.py:227
  35.2 0.5 collective-permute-done.2
  35.7 1.2 collective-permute-done.1
  36.9 1.5 %fusion.10 = f32[512]{0:T(512)S(1)} fusion(bf16[256,1024]{1,0:T(8,128)(2,1)} %bitcast.10, bf16[256,1024]{1,0:T(8,128)(2,1)} %bitcast.9), kind=kLoop, calls=%fused_computation.15 | loop fusion | flops 3145216 | bytes 1050624 | tf_op jit(solution)/shard_map/reduce_sum | solution.py:22
  38.4 5.0 %fusion.4.kt_ref.vt_ref.kb_ref.vb_ref = bf16[512,2048]{1,0:T(8,128)(2,1)} fusion(bf16[1024,3072]{1,0:T(8,128)(2,1)S(1)} %bitcast.57, f32[512]{0:T(512)S(1)} %add_rsqrt_fusion.3, f32[1024]{0:T(1024)S(1)} %copy-done.4, bf16[256,1024]{1,0:T(8,128)(2,1)} %bitcast.10, bf16[256,1024]{1,0:T(8,128)(2,1)} %bitcast.9), kind=kOutput, calls=%fused_computation.9 | convolution fusion | flops 2152202240 | bytes 7346176 | tf_op jit(solution)/shard_map/dot_general | solution.py:229
  43.4 21.3 %spatial.1 = bf16[512,1024]{1,0:T(8,128)(2,1)} custom-call(s32[2]{0:T(128)} %bitcast.55, s32[1]{0:T(128)} %bitcast.7.first_ref, bf16[512,3072]{1,0:T(8,128)(2,1)} %convolution_convert_fusion.1.q_ref.k_ref.v_ref, bf16[512,3072]{1,0:T(8,128)(2,1)} %convolution_convert_fusion.1.q_ref.k_ref.v_ref, bf16[512,3072]{1,0:T(8,128)(2,1)} %convolution_convert_fusion.1.q_ref.k_ref.v_ref, ...), custom_call_target="tpu_custom_call" | custom-call | flops 1610612736 | bytes 6291456 | tf_op jit(solution)/shard_map/spatial/pallas_call | solution.py:82
  64.7 0.0 copy-start.8
  64.7 0.0 slice-start.2
  64.7 2.8 %fusion.16 = (f32[512]{0:T(512)S(1)}, bf16[512,1024]{1,0:T(8,128)(2,1)S(1)}) fusion(bf16[512,1024]{1,0:T(8,128)(2,1)} %spatial.1, bf16[1024,1024]{1,0:T(8,128)(2,1)S(1)} %copy-done, bf16[2,8,2,16,1024]{4,3,2,1,0:T(8,128)(2,1)S(1)} %copy-done.2), kind=kOutput, calls=%fused_computation.21 | convolution fusion | flops 1076887040 | bytes 5244928 | tf_op jit(solution)/shard_map/dot_general | solution.py:232
  67.5 1.5 %collective-permute-start.3 = (bf16[512,1024]{1,0:T(8,128)(2,1)S(1)}, bf16[512,1024]{1,0:T(8,128)(2,1)S(1)}, u32[]{:S(2)}, u32[]{:S(2)}) collective-permute-start(bf16[512,1024]{1,0:T(8,128)(2,1)S(1)} %get-tuple-element.20), channel_id=1, source_target_pairs={{0,4},{4,0},{1,5},{5,1},{2,6},{6,2},{3,7},{7,3},{8,12},{12,8},{9,1... | collective-permute-start | bytes 3145736 | tf_op jit(solution)/shard_map/ppermute | solution.py:236
  69.0 7.9 %convolution_convert_fusion = bf16[512,3072]{1,0:T(8,128)(2,1)} fusion(bf16[1024,3072]{1,0:T(8,128)(2,1)} %param.17, bf16[512,1024]{1,0:T(8,128)(2,1)S(1)} %get-tuple-element.20, f32[1024]{0:T(1024)S(1)} %copy-done.8, f32[512]{0:T(512)S(1)} %add_rsqrt_fusion.2), kind=kOutput, calls=%fused_computation | convolution fusion | flops 3224895488 | bytes 10491904 | tf_op jit(solution)/shard_map/dot_general | solution.py:237
  76.9 13.9 %collective-permute-done.3 = bf16[512,1024]{1,0:T(8,128)(2,1)S(1)} collective-permute-done((bf16[512,1024]{1,0:T(8,128)(2,1)S(1)}, bf16[512,1024]{1,0:T(8,128)(2,1)S(1)}, u32[]{:S(2)}, u32[]{:S(2)}) %collective-permute-start.3) | collective-permute-done | bytes 1048608 | tf_op jit(solution)/shard_map/ppermute | solution.py:236
  90.8 0.3 fusion.13
  91.1 3.8 %fusion.7 = bf16[512,2048]{1,0:T(8,128)(2,1)} fusion(bf16[1024,3072]{1,0:T(8,128)(2,1)S(1)} %bitcast.59, bf16[512,1024]{1,0:T(8,128)(2,1)S(1)} %collective-permute-done.3, f32[512]{0:T(512)S(1)} %add_rsqrt_fusion.1, f32[1024]{0:T(1024)S(1)} %copy-done.8), kind=kOutput, calls=%fused_computation.10 | convolution fusion | flops 2150629376 | bytes 7346176 | tf_op jit(solution)/shard_map/dot_general | solution.py:238
  94.9 7.0 %temporal.1 = bf16[2,256,1024]{2,1,0:T(8,128)(2,1)} custom-call(s32[2]{0:T(128)} %copy-done.5, s32[4]{0:T(128)} %pad_add_fusion.k_order, bf16[1024,128]{1,0:T(8,128)(2,1)} %fusion.35.gather_ref, bf16[128,1024]{1,0:T(8,128)(2,1)} %fusion.36.spread_ref, bf16[2,256,3072]{2,1,0:T(8,128)(2,1)} %bitcast.47, bf16[2,256,3072]{2,1,0:T(8,128)(2,1)} %bitcast.48, ...), custom_call_target="tpu_custom_call" | custom-call | flops 1073741824 | bytes 4194304 | tf_op jit(solution)/shard_map/temporal/pallas_call | solution.py:134
  101.9 2.5 %convolution_convert_fusion.2 = bf16[1024,1024]{0,1:T(8,128)(2,1)S(1)} fusion(bf16[512,1024]{1,0:T(8,128)(2,1)} %bitcast.53, bf16[512,1024]{1,0:T(8,128)(2,1)S(1)} %bitcast.60), kind=kOutput, calls=%fused_computation.33 | convolution fusion | flops 1074790400 | bytes 4194304 | tf_op jit(solution)/shard_map/dot_general | solution.py:241
  104.5 1.3 copy-done.3
  105.8 0.1 constant_dynamic-slice_fusion.4
  105.9 0.1 collective-permute-start.4
  106.0 2.8 %collective-permute-done.4 = bf16[1024,512]{0,1:T(8,128)(2,1)} collective-permute-done((bf16[1024,512]{0,1:T(8,128)(2,1)S(1)}, bf16[1024,512]{0,1:T(8,128)(2,1)}, u32[]{:S(2)}, u32[]{:S(2)}) %collective-permute-start.4) | collective-permute-done | bytes 1048608 | tf_op jit(solution)/shard_map/ppermute | solution.py:155
  108.7 1.9 %add_convert_fusion = bf16[1024,512]{0,1:T(8,128)(2,1)S(1)} fusion(bf16[1024,512]{0,1:T(8,128)(2,1)} %collective-permute-done.4, bf16[1024,1024]{0,1:T(8,128)(2,1)} %copy-done.3, s32[]{:T(128)S(6)} %select_n.242), kind=kLoop, calls=%fused_computation.32 | loop fusion | flops 2097152 | bytes 3145732 | tf_op jit(solution)/shard_map/convert_element_type | solution.py:164
  110.7 0.1 fusion.47
  110.8 1.3 collective-permute-start.7
  112.0 1.6 %collective-permute-start.5 = (bf16[1024,128]{0,1:T(8,128)(2,1)S(1)}, bf16[1024,128]{0,1:T(8,128)(2,1)S(1)}, u32[]{:S(2)}, u32[]{:S(2)}) collective-permute-start(bf16[1024,128]{0,1:T(8,128)(2,1)S(1)} %constant_dynamic-slice_fusion.3), channel_id=1, source_target_pairs={{0,16},{8,24},{16,0},{24,8},{1,17},{9,25},{17,1},{25,9},{2,18},{10... | collective-permute-start | bytes 786440 | tf_op jit(solution)/shard_map/ppermute | solution.py:155
  113.6 5.7 %collective-permute-done.7 = bf16[512,256]{0,1:T(8,128)(2,1)} collective-permute-done((bf16[512,256]{0,1:T(8,128)(2,1)S(1)}, bf16[512,256]{0,1:T(8,128)(2,1)}, u32[]{:S(2)}, u32[]{:S(2)}) %collective-permute-start.7) | collective-permute-done | bytes 262176 | tf_op jit(solution)/shard_map/ppermute | solution.py:173
  119.3 1.0 add_convert_fusion.1
  120.3 1.3 collective-permute-start.8
  121.6 0.0 collective-permute-done.5
  121.6 0.1 add_convert_fusion.2
  121.7 1.6 %collective-permute-start.6 = (bf16[512,128]{0,1:T(8,128)(2,1)S(1)}, bf16[512,128]{0,1:T(8,128)(2,1)S(1)}, u32[]{:S(2)}, u32[]{:S(2)}) collective-permute-start(bf16[512,128]{0,1:T(8,128)(2,1)S(1)} %constant_dynamic-slice_fusion.2), channel_id=1, source_target_pairs={{0,4},{4,0},{1,5},{5,1},{2,6},{6,2},{3,7},{7,3},{8,12},{12,8},{9,1... | collective-permute-start | bytes 393224 | tf_op jit(solution)/shard_map/ppermute | solution.py:173
  123.3 2.1 %collective-permute-done.8 = bf16[512,128]{0,1:T(8,128)(2,1)S(1)} collective-permute-done((bf16[512,128]{0,1:T(8,128)(2,1)S(1)}, bf16[512,128]{0,1:T(8,128)(2,1)S(1)}, u32[]{:S(2)}, u32[]{:S(2)}) %collective-permute-start.8) | collective-permute-done | bytes 131104 | tf_op jit(solution)/shard_map/ppermute | solution.py:155
  125.4 1.3 collective-permute-done.6
  126.9 3.6 %collective-permute-start.10 = (bf16[128,256]{0,1:T(8,128)(2,1)S(1)}, bf16[128,256]{0,1:T(8,128)(2,1)S(1)}, u32[]{:S(2)}, u32[]{:S(2)}) collective-permute-start(bf16[128,256]{0,1:T(8,128)(2,1)S(1)} %get-tuple-element.15), channel_id=1, source_target_pairs={{0,2},{1,3},{2,0},{3,1},{4,6},{5,7},{6,4},{7,5},{8,10},{9,11},{10,... | collective-permute-start | bytes 196616 | tf_op jit(solution)/shard_map/ppermute | solution.py:173
  130.4 1.9 %collective-permute-start.11 = (bf16[128,256]{0,1:T(8,128)(2,1)S(1)}, bf16[128,256]{0,1:T(8,128)(2,1)S(1)}, u32[]{:S(2)}, u32[]{:S(2)}) collective-permute-start(bf16[128,256]{0,1:T(8,128)(2,1)S(1)} %get-tuple-element.16), channel_id=1, source_target_pairs={{0,3},{1,0},{2,1},{3,2},{4,7},{5,4},{6,5},{7,6},{8,11},{9,8},{10,9... | collective-permute-start | bytes 196616 | tf_op jit(solution)/shard_map/ppermute | solution.py:173
  132.3 0.5 collective-permute-start.9
  132.8 2.7 %collective-permute-done.11 = bf16[128,256]{0,1:T(8,128)(2,1)S(1)} collective-permute-done((bf16[128,256]{0,1:T(8,128)(2,1)S(1)}, bf16[128,256]{0,1:T(8,128)(2,1)S(1)}, u32[]{:S(2)}, u32[]{:S(2)}) %collective-permute-start.11) | collective-permute-done | bytes 65568 | tf_op jit(solution)/shard_map/ppermute | solution.py:173
  135.5 2.8 %collective-permute-done.9 = bf16[128,256]{0,1:T(8,128)(2,1)S(1)} collective-permute-done((bf16[128,256]{0,1:T(8,128)(2,1)S(1)}, bf16[128,256]{0,1:T(8,128)(2,1)S(1)}, u32[]{:S(2)}, u32[]{:S(2)}) %collective-permute-start.9) | collective-permute-done | bytes 65568 | tf_op jit(solution)/shard_map/ppermute | solution.py:173
  138.4 0.1 collective-permute-start.12
  138.5 0.6 collective-permute-start.13
  139.0 1.3 collective-permute-start.14
  140.3 4.4 %fusion.19 = bf16[512,1024]{1,0:T(8,128)(2,1)} fusion(bf16[512,1024]{1,0:T(8,128)(2,1)} %copy-done.7, bf16[512,1024]{1,0:T(8,128)(2,1)} %bitcast.54, bf16[1024,1024]{1,0:T(8,128)(2,1)} %param.18), kind=kOutput, calls=%fused_computation.24 | convolution fusion | flops 1075314688 | bytes 5242880 | tf_op jit(solution)/shard_map/dot_general | solution.py:244
  144.7 0.0 collective-permute-done.12
  144.7 0.0 collective-permute-done.13
  144.7 0.0 collective-permute-done.14
  144.9 0.9 copy.13
  (44 shorter events, 0.4 us)
Async XLA Ops:
  0.6 64.1 %copy-start = (bf16[1024,1024]{1,0:T(8,128)(2,1)S(1)}, bf16[1024,1024]{1,0:T(8,128)(2,1)}, u32[]{:S(2)}) copy-start(bf16[1024,1024]{1,0:T(8,128)(2,1)} %param.15) | copy-start | bytes 6291460
  1.9 15.1 %collective-permute-start = (bf16[2,8,16,1024]{3,2,1,0:T(8,128)(2,1)S(1)}, bf16[2,8,16,1024]{3,2,1,0:T(8,128)(2,1)}, u32[]{:S(2)}, u32[]{:S(2)}) collective-permute-start(bf16[2,8,16,1024]{3,2,1,0:T(8,128)(2,1)S(1)} %dynamic-slice_bitcast_fusion), channel_id=1, source_target_pairs={{0,4},{4,0},{1,5},{5,1},{2,6},{6,2},{3,7},{7,3},{8,12},{12,8},{9,1... | collective-permute-start | bytes 1572872 | tf_op jit(solution)/shard_map/ppermute | solution.py:218
  5.7 12.6 %copy-start.5 = (s32[2]{0:T(128)}, s32[2]{0:T(128)S(1)}, u32[]{:S(2)}) copy-start(s32[2]{0:T(128)S(1)} %get-tuple-element.18.q_order) | copy-start | bytes 28
  18.4 1.0 copy-start.1
  18.4 8.8 %copy-start.4 = (f32[1024]{0:T(1024)S(1)}, f32[1024]{0:T(1024)}, u32[]{:S(2)}) copy-start(f32[1024]{0:T(1024)} %param.13) | copy-start | bytes 12292
  20.4 15.3 %collective-permute-start.2 = (bf16[2,4,32,1024]{3,2,1,0:T(8,128)(2,1)}, bf16[2,4,32,1024]{3,2,1,0:T(8,128)(2,1)}, u32[]{:S(2)}, u32[]{:S(2)}) collective-permute-start(bf16[2,4,32,1024]{3,2,1,0:T(8,128)(2,1)} %get-tuple-element.9), channel_id=1, source_target_pairs={{1,0},{2,1},{3,2},{5,4},{6,5},{7,6},{9,8},{10,9},{11,10},{13,12},{... | collective-permute-start | bytes 1572872 | tf_op jit(solution)/shard_map/ppermute | solution.py:225
  21.7 15.2 %collective-permute-start.1 = (bf16[2,4,32,1024]{3,2,1,0:T(8,128)(2,1)}, bf16[2,4,32,1024]{3,2,1,0:T(8,128)(2,1)}, u32[]{:S(2)}, u32[]{:S(2)}) collective-permute-start(bf16[2,4,32,1024]{3,2,1,0:T(8,128)(2,1)} %get-tuple-element.8), channel_id=1, source_target_pairs={{0,1},{1,2},{2,3},{4,5},{5,6},{6,7},{8,9},{9,10},{10,11},{12,13},{... | collective-permute-start | bytes 1572872 | tf_op jit(solution)/shard_map/ppermute | solution.py:224
  27.1 11.2 %slice-start = ((s8[6291456]{0:T(1024)(128)(4,1)}), s8[4194304]{0:T(1024)(128)(4,1)S(1)}, s32[]{:S(2)}) async-start(s8[6291456]{0:T(1024)(128)(4,1)} %bitcast.56), calls=%async_computation | async-start | bytes 8388608
  27.5 10.9 %slice-start.1 = ((s8[6291456]{0:T(1024)(128)(4,1)}), s8[2097152]{0:T(1024)(128)(4,1)S(1)}, s32[]{:S(2)}) async-start(s8[6291456]{0:T(1024)(128)(4,1)} %bitcast.56), calls=%async_computation.1 | async-start | bytes 4194304
  43.4 21.3 %copy-start.2 = (bf16[2,8,2,16,1024]{4,3,2,1,0:T(8,128)(2,1)S(1)}, bf16[2,8,2,16,1024]{4,3,2,1,0:T(8,128)(2,1)}, u32[]{:S(2)}) copy-start(bf16[2,8,2,16,1024]{4,3,2,1,0:T(8,128)(2,1)} %copy-done.1) | copy-start | bytes 3145732
  64.7 4.3 %copy-start.8 = (f32[1024]{0:T(1024)S(1)}, f32[1024]{0:T(1024)}, u32[]{:S(2)}) copy-start(f32[1024]{0:T(1024)} %param.16) | copy-start | bytes 12292
  64.7 26.3 %slice-start.2 = ((s8[6291456]{0:T(1024)(128)(4,1)}), s8[4194304]{0:T(1024)(128)(4,1)S(1)}, s32[]{:S(2)}) async-start(s8[6291456]{0:T(1024)(128)(4,1)} %bitcast.58), calls=%async_computation.2 | async-start | bytes 8388608
  67.5 9.4 %copy-start.7 = (bf16[512,1024]{1,0:T(8,128)(2,1)}, bf16[512,1024]{1,0:T(8,128)(2,1)S(1)}, u32[]{:S(2)}) copy-start(bf16[512,1024]{1,0:T(8,128)(2,1)S(1)} %get-tuple-element.20) | copy-start | bytes 3145732
  67.5 23.2 %collective-permute-start.3 = (bf16[512,1024]{1,0:T(8,128)(2,1)S(1)}, bf16[512,1024]{1,0:T(8,128)(2,1)S(1)}, u32[]{:S(2)}, u32[]{:S(2)}) collective-permute-start(bf16[512,1024]{1,0:T(8,128)(2,1)S(1)} %get-tuple-element.20), channel_id=1, source_target_pairs={{0,4},{4,0},{1,5},{5,1},{2,6},{6,2},{3,7},{7,3},{8,12},{12,8},{9,1... | collective-permute-start | bytes 3145736 | tf_op jit(solution)/shard_map/ppermute | solution.py:236
  69.0 22.0 %slice-start.3 = ((s8[6291456]{0:T(1024)(128)(4,1)}), s8[2097152]{0:T(1024)(128)(4,1)S(1)}, s32[]{:S(2)}) async-start(s8[6291456]{0:T(1024)(128)(4,1)} %bitcast.58), calls=%async_computation.3 | async-start | bytes 4194304
  94.9 7.0 %copy-start.6 = (bf16[1,2,8,32,1024]{4,3,2,1,0:T(8,128)(2,1)S(1)}, bf16[1,2,8,32,1024]{4,3,2,1,0:T(8,128)(2,1)}, u32[]{:S(2)}) copy-start(bf16[1,2,8,32,1024]{4,3,2,1,0:T(8,128)(2,1)} %param.19) | copy-start | bytes 3145732
  104.5 1.3 copy-start.3
  105.9 2.9 %collective-permute-start.4 = (bf16[1024,512]{0,1:T(8,128)(2,1)S(1)}, bf16[1024,512]{0,1:T(8,128)(2,1)}, u32[]{:S(2)}, u32[]{:S(2)}) collective-permute-start(bf16[1024,512]{0,1:T(8,128)(2,1)S(1)} %constant_dynamic-slice_fusion.4), channel_id=1, source_target_pairs={{0,8},{8,0},{16,24},{24,16},{1,9},{9,1},{17,25},{25,17},{2,10},{10... | collective-permute-start | bytes 3145736 | tf_op jit(solution)/shard_map/ppermute | solution.py:155
  110.8 8.5 %collective-permute-start.7 = (bf16[512,256]{0,1:T(8,128)(2,1)S(1)}, bf16[512,256]{0,1:T(8,128)(2,1)}, u32[]{:S(2)}, u32[]{:S(2)}) collective-permute-start(bf16[512,256]{0,1:T(8,128)(2,1)S(1)} %constant_dynamic-slice_fusion.1), channel_id=1, source_target_pairs={{0,4},{4,0},{1,5},{5,1},{2,6},{6,2},{3,7},{7,3},{8,12},{12,8},{9,1... | collective-permute-start | bytes 786440 | tf_op jit(solution)/shard_map/ppermute | solution.py:173
  112.0 9.6 %collective-permute-start.5 = (bf16[1024,128]{0,1:T(8,128)(2,1)S(1)}, bf16[1024,128]{0,1:T(8,128)(2,1)S(1)}, u32[]{:S(2)}, u32[]{:S(2)}) collective-permute-start(bf16[1024,128]{0,1:T(8,128)(2,1)S(1)} %constant_dynamic-slice_fusion.3), channel_id=1, source_target_pairs={{0,16},{8,24},{16,0},{24,8},{1,17},{9,25},{17,1},{25,9},{2,18},{10... | collective-permute-start | bytes 786440 | tf_op jit(solution)/shard_map/ppermute | solution.py:155
  120.3 5.0 %collective-permute-start.8 = (bf16[512,128]{0,1:T(8,128)(2,1)S(1)}, bf16[512,128]{0,1:T(8,128)(2,1)S(1)}, u32[]{:S(2)}, u32[]{:S(2)}) collective-permute-start(bf16[512,128]{0,1:T(8,128)(2,1)S(1)} %constant_dynamic-slice_fusion), channel_id=1, source_target_pairs={{0,16},{8,24},{16,0},{24,8},{1,17},{9,25},{17,1},{25,9},{2,18},{10... | collective-permute-start | bytes 393224 | tf_op jit(solution)/shard_map/ppermute | solution.py:155
  121.7 5.0 %collective-permute-start.6 = (bf16[512,128]{0,1:T(8,128)(2,1)S(1)}, bf16[512,128]{0,1:T(8,128)(2,1)S(1)}, u32[]{:S(2)}, u32[]{:S(2)}) collective-permute-start(bf16[512,128]{0,1:T(8,128)(2,1)S(1)} %constant_dynamic-slice_fusion.2), channel_id=1, source_target_pairs={{0,4},{4,0},{1,5},{5,1},{2,6},{6,2},{3,7},{7,3},{8,12},{12,8},{9,1... | collective-permute-start | bytes 393224 | tf_op jit(solution)/shard_map/ppermute | solution.py:173
  126.9 5.9 %collective-permute-start.10 = (bf16[128,256]{0,1:T(8,128)(2,1)S(1)}, bf16[128,256]{0,1:T(8,128)(2,1)S(1)}, u32[]{:S(2)}, u32[]{:S(2)}) collective-permute-start(bf16[128,256]{0,1:T(8,128)(2,1)S(1)} %get-tuple-element.15), channel_id=1, source_target_pairs={{0,2},{1,3},{2,0},{3,1},{4,6},{5,7},{6,4},{7,5},{8,10},{9,11},{10,... | collective-permute-start | bytes 196616 | tf_op jit(solution)/shard_map/ppermute | solution.py:173
  130.4 5.1 %collective-permute-start.11 = (bf16[128,256]{0,1:T(8,128)(2,1)S(1)}, bf16[128,256]{0,1:T(8,128)(2,1)S(1)}, u32[]{:S(2)}, u32[]{:S(2)}) collective-permute-start(bf16[128,256]{0,1:T(8,128)(2,1)S(1)} %get-tuple-element.16), channel_id=1, source_target_pairs={{0,3},{1,0},{2,1},{3,2},{4,7},{5,4},{6,5},{7,6},{8,11},{9,8},{10,9... | collective-permute-start | bytes 196616 | tf_op jit(solution)/shard_map/ppermute | solution.py:173
  132.3 6.1 %collective-permute-start.9 = (bf16[128,256]{0,1:T(8,128)(2,1)S(1)}, bf16[128,256]{0,1:T(8,128)(2,1)S(1)}, u32[]{:S(2)}, u32[]{:S(2)}) collective-permute-start(bf16[128,256]{0,1:T(8,128)(2,1)S(1)} %get-tuple-element.14), channel_id=1, source_target_pairs={{0,1},{1,2},{2,3},{3,0},{4,5},{5,6},{6,7},{7,4},{8,9},{9,10},{10,1... | collective-permute-start | bytes 196616 | tf_op jit(solution)/shard_map/ppermute | solution.py:173
  138.4 6.3 %collective-permute-start.12 = (bf16[128,256]{0,1:T(8,128)(2,1)S(1)}, bf16[128,256]{0,1:T(8,128)(2,1)S(1)}, u32[]{:S(2)}, u32[]{:S(2)}) collective-permute-start(bf16[128,256]{0,1:T(8,128)(2,1)S(1)} %add_convert_fusion.5), channel_id=1, source_target_pairs={{0,8},{8,0},{16,24},{24,16},{1,9},{9,1},{17,25},{25,17},{2,10},{10... | collective-permute-start | bytes 196616 | tf_op jit(solution)/shard_map/ppermute | solution.py:155
  138.5 6.2 %collective-permute-start.13 = (bf16[128,256]{0,1:T(8,128)(2,1)S(1)}, bf16[128,256]{0,1:T(8,128)(2,1)S(1)}, u32[]{:S(2)}, u32[]{:S(2)}) collective-permute-start(bf16[128,256]{0,1:T(8,128)(2,1)S(1)} %add_convert_fusion.5), channel_id=1, source_target_pairs={{0,16},{8,24},{16,0},{24,8},{1,17},{9,25},{17,1},{25,9},{2,18},{10... | collective-permute-start | bytes 196616 | tf_op jit(solution)/shard_map/ppermute | solution.py:155
  139.0 5.7 %collective-permute-start.14 = (bf16[128,256]{0,1:T(8,128)(2,1)S(1)}, bf16[128,256]{0,1:T(8,128)(2,1)S(1)}, u32[]{:S(2)}, u32[]{:S(2)}) collective-permute-start(bf16[128,256]{0,1:T(8,128)(2,1)S(1)} %add_convert_fusion.5), channel_id=1, source_target_pairs={{0,24},{8,16},{16,8},{24,0},{1,25},{9,17},{17,9},{25,1},{2,26},{10... | collective-permute-start | bytes 196616 | tf_op jit(solution)/shard_map/ppermute | solution.py:155

commit v2 on v1

--- a/solution.py
+++ b/solution.py
@@ -50,23 +50,20 @@
     lane = lax.broadcasted_iota(jnp.int32, (1, LANES), 1)
     first_head = (lane < HEAD_DIM).astype(F32)
     masks = (first_head.astype(BF), (1.0 - first_head).astype(BF))
+    ones = jnp.ones((window, LANES), BF)
     for pair in range(q_ref.shape[1] // LANES):
         at = slice(pair * LANES, (pair + 1) * LANES)
         for chunk in range(chunks):
             here = slice(chunk * span, (chunk + 1) * span)
             near = slice(chunk * span, chunk * span + window)
             q = q_ref[here, at] * BF(SCALE)
-            k = kx[near, at]
-            v = vx[near, at]
-            outs = []
-            for head in range(2):
-                s = lax.dot_general(q * masks[head], k, (((1,), (1,)), ((), ())),
-                                    preferred_element_type=F32) + bias[chunk]
-                top_score = jnp.max(s, axis=-1, keepdims=True)
-                p = jnp.exp(s - top_score).astype(BF)
-                o = jnp.dot(p, v * masks[head] + masks[1 - head], preferred_element_type=F32)
-                outs.append(o / pltpu.roll(o, HEAD_DIM, 1))
-            o_ref[here, at] = jnp.where(lane < HEAD_DIM, outs[0], outs[1]).astype(BF)
+            both = jnp.concatenate([q * masks[0], q * masks[1]], axis=0)
+            s = lax.dot_general(both, kx[near, at], (((1,), (1,)), ((), ())), preferred_element_type=F32)
+            s = s + jnp.concatenate([bias[chunk], bias[chunk]], axis=0)
+            p = jnp.exp(s - jnp.max(s, axis=-1, keepdims=True)).astype(BF)
+            o = jnp.dot(p, jnp.concatenate([vx[near, at], ones], axis=1), preferred_element_type=F32)
+            o = o[:, :LANES] / o[:, LANES:]
+            o_ref[here, at] = jnp.where(lane < HEAD_DIM, o[:span], o[span:]).astype(BF)
 
 
 def spatial_attend(projected, halo, reach, first_row, frames, rows, cols, all_rows):
@@ -96,52 +93,45 @@
     )(reach, first_row, projected, projected, projected, halo, halo, halo, halo)
 
 
-def temporal_kernel(others, q_order, k_order, gather_ref, spread_ref, q_ref, *refs):
-    k_refs, v_refs, o_ref = refs[:others + 1], refs[others + 1:2 * others + 2], refs[-1]
-    frames = q_ref.shape[0]
-    keys = [(ref, i) for ref in k_refs for i in range(frames)]
-    values = [(ref, i) for ref in v_refs for i in range(frames)]
+def temporal_kernel(frames, keys, q_order, k_order, gather_ref, spread_ref, *refs):
+    q_refs, k_refs, v_refs, o_ref = refs[:frames], refs[frames:frames + keys], refs[frames + keys:-1], refs[-1]
     for f in range(frames):
-        q = q_ref[f] * BF(SCALE)
+        q = q_refs[f][...] * BF(SCALE)
         scores = []
-        for g, (ref, i) in enumerate(keys):
-            s = jnp.dot(q * ref[i], gather_ref[...], preferred_element_type=F32)
+        for g in range(keys):
+            s = jnp.dot(q * k_refs[g][...], gather_ref[...], preferred_element_type=F32)
             scores.append(s + jnp.where(k_order[g] <= q_order[f], 0.0, -1e30))
         top_score = functools.reduce(jnp.maximum, scores)
         exps = [jnp.exp(s - top_score) for s in scores]
         scale = 1.0 / functools.reduce(jnp.add, exps)
         total = None
-        for g, (ref, i) in enumerate(values):
+        for g in range(keys):
             w = jnp.dot((exps[g] * scale).astype(BF), spread_ref[...], preferred_element_type=F32)
-            term = w * ref[i].astype(F32)
+            term = w * v_refs[g][...].astype(F32)
             total = term if total is None else total + term
         o_ref[f] = total.astype(BF)
 
 
-def temporal_attend(own, others, q_order, k_order, frames):
-    depth = own.shape[1] // 3
-    tokens = own.shape[0] // frames
+def temporal_attend(own, others, q_order, k_order):
+    frames, keys = len(own), len(own) + len(others)
+    tokens, depth = own[0].shape[0], own[0].shape[1] // 3
     size = min(tokens, 64)
     head = jnp.arange(depth, dtype=jnp.int32) // HEAD_DIM
     gather = (head[:, None] == jnp.arange(LANES, dtype=jnp.int32)[None, :]).astype(BF)
-    own = own.reshape(frames, tokens, 3 * depth)
-    others = [value.reshape(frames, tokens, 2 * depth) for value in others]
-    part = lambda column: pl.BlockSpec((frames, size, depth), lambda i: (0, i, column))
+    part = lambda column: pl.BlockSpec((size, depth), lambda i: (i, column))
     smem = pl.BlockSpec(memory_space=pltpu.SMEM)
     whole = lambda shape: pl.BlockSpec(shape, lambda i: (0, 0))
-    count = len(others)
-    keys = (count + 1) * frames
     out = pl.pallas_call(
-        functools.partial(temporal_kernel, count),
+        functools.partial(temporal_kernel, frames, keys),
         grid=(tokens // size,),
         out_shape=jax.ShapeDtypeStruct((frames, tokens, depth), BF),
-        in_specs=[smem, smem, whole((depth, LANES)), whole((LANES, depth)), part(0)]
-        + [part(1)] + [part(0)] * count + [part(2)] + [part(1)] * count,
-        out_specs=part(0),
+        in_specs=[smem, smem, whole((depth, LANES)), whole((LANES, depth))] + [part(0)] * frames
+        + [part(1)] * frames + [part(0)] * len(others) + [part(2)] * frames + [part(1)] * len(others),
+        out_specs=pl.BlockSpec((frames, size, depth), lambda i: (0, i, 0)),
         cost_estimate=pl.CostEstimate(flops=4 * frames * keys * tokens * depth * LANES,
                                       bytes_accessed=4 * keys * tokens * depth, transcendentals=0),
         name="temporal",
-    )(q_order, k_order, gather, gather.T, own, own, *others, own, *others)
+    )(q_order, k_order, gather, gather.T, *own, *own, *others, *own, *others)
     return out.reshape(frames * tokens, depth)
 
 
@@ -212,32 +202,44 @@
     frames, cols = all_frames // ranks, part_cols * ranks
     tokens, span = rows * cols, HALO * cols
     clip = clip_tokens[0]
-    pieces = []
-    for shift in range(ranks):
-        block = lax.dynamic_slice_in_dim(clip, (me + shift) % ranks * frames, frames, 0)
-        pieces.append(lax.ppermute(block, "tm", cyclic("tm", shift)) if shift else block)
-    here = jnp.stack([lax.select_n((me - j) % ranks, *pieces) if ranks > 2 else
-                      jnp.where(me == j, pieces[0], pieces[1]) for j in range(ranks)], axis=2)
-    here = here.reshape(frames, rows, cols, depth)
     up = [(i, i + 1) for i in range(places - 1)]
     down = [(i + 1, i) for i in range(places - 1)]
-    above = lax.ppermute(here[:, rows - HALO:], "space", up).reshape(frames * span, depth)
-    below = lax.ppermute(here[:, :HALO], "space", down).reshape(frames * span, depth)
-    flat = here.reshape(frames * tokens, depth)
-    projected = jnp.dot(normalize(flat, spatial_gain), spatial_heads, preferred_element_type=F32).astype(BF)
-    halo = normalize(jnp.concatenate([above, below]), spatial_gain)
-    halo = jnp.dot(halo, spatial_heads[:, depth:], preferred_element_type=F32).astype(BF)
     first_row = (place * rows).astype(jnp.int32).reshape(1)
-    context = spatial_attend(projected, halo, row_reach.reshape(-1), first_row, frames, rows, cols, rows * places)
-    middle = (flat.astype(F32) + jnp.dot(context, spatial_merge, preferred_element_type=F32)).astype(BF)
+    reach = row_reach.reshape(-1)
+
+    def project(values, gain, weights):
+        normed = lax.optimization_barrier(normalize(values, gain))
+        return jnp.dot(normed, weights, preferred_element_type=F32).astype(BF)
+
+    staged = []
+    for f in range(frames):
+        pieces = []
+        for shift in range(ranks):
+            block = lax.dynamic_index_in_dim(clip, (me + shift) % ranks * frames + f, 0, keepdims=False)
+            pieces.append(lax.ppermute(block, "tm", cyclic("tm", shift)) if shift else block)
+        here = jnp.stack([lax.select_n((me - j) % ranks, *pieces) if ranks > 2 else
+                          jnp.where(me == j, pieces[0], pieces[1]) for j in range(ranks)], axis=1)
+        here = here.reshape(rows, cols, depth)
+        above = lax.ppermute(here[rows - HALO:], "space", up).reshape(span, depth)
+        below = lax.ppermute(here[:HALO], "space", down).reshape(span, depth)
+        flat = here.reshape(tokens, depth)
+        projected = project(flat, spatial_gain, spatial_heads)
+        halo = project(jnp.concatenate([above, below]), spatial_gain, spatial_heads[:, depth:])
+        staged.append((flat, projected, halo))
+    middles = []
+    for f, (flat, projected, halo) in enumerate(staged):
+        if f:
+            middles[-1], projected = lax.optimization_barrier((middles[-1], projected))
+        context = spatial_attend(projected, halo, reach[f:f + 1], first_row, 1, rows, cols, rows * places)
+        middles.append((flat.astype(F32) + jnp.dot(context, spatial_merge, preferred_element_type=F32)).astype(BF))
 
     order = frame_order.reshape(-1)
     orders = [lax.dynamic_slice_in_dim(order, (me - shift) % ranks * frames, frames, 0) for shift in range(ranks)]
-    arrived = [lax.ppermute(middle, "tm", cyclic("tm", shift)) for shift in range(1, ranks)]
-    own = jnp.dot(normalize(middle, temporal_gain), temporal_heads, preferred_element_type=F32).astype(BF)
-    others = [jnp.dot(normalize(value, temporal_gain), temporal_heads[:, depth:],
-                      preferred_element_type=F32).astype(BF) for value in arrived]
-    context = temporal_attend(own, others, orders[0], jnp.concatenate(orders), frames)
+    arrived = [lax.ppermute(value, "tm", cyclic("tm", shift)) for shift in range(1, ranks) for value in middles]
+    own = [project(value, temporal_gain, temporal_heads) for value in middles]
+    others = [project(value, temporal_gain, temporal_heads[:, depth:]) for value in arrived]
+    context = temporal_attend(own, others, orders[0], jnp.concatenate(orders))
+    middle = jnp.concatenate(middles)
     part = lax.dot_general(context, cotangent.reshape(-1, depth), (((0,), (0,)), ((), ())),
                            preferred_element_type=F32).astype(BF)
     weight_grad = reduce_gradient(part)

time: 146 us -> 163 us (1.12)
  other arithmetic: 9.26 us -> 18.5 us
  Pallas kernels: 28.3 us -> 21.7 us
  starting transfers between devices: 24.8 us -> 29.9 us
  matrix products: 34.1 us -> 38.4 us
  local copies, waits for them, and re-layouts: 6.47 us -> 9.03 us
    pallas_call x1 -> x2, Pallas kernels: 21.3 us -> 14.4 us  [spatial_attend(): pl.pallas_call(functools.partial(spatial_kernel, rows, cols, all_rows), g...]
    ppermute x3 -> x6, starting transfers between devices: 8.15 us -> 13.6 us  [the longest x2 8.98 us: per_device(): above = lax.ppermute(here[rows - HALO:], 'space', up).reshape(span, depth)]
    ppermute x3 -> x6, waiting for transfers between devices: 15.5 us -> 20.3 us  [the longest x2 18.1 us: per_device(): lax.ppermute(value, 'tm', cyclic('tm', shift))]
    convert_element_type x1 -> x2, other arithmetic: 0.31 us -> 4.21 us  [normalize(): return (scaled * gain_vector).astype(BF)]
    ppermute x5, waiting for transfers between devices: 12.6 us -> 9.72 us  [scatter_rows(): arrived = lax.ppermute(take((me + shift) % n), axis, cyclic(axis, shift))]
    dot_general x1 -> x2, matrix products: 2.76 us -> 5.56 us  [per_device(): jnp.dot(context, spatial_merge, preferred_element_type=F32)]
    reduce_sum x3 -> x7, other arithmetic: 2.04 us -> 4.48 us  [normalize(): jnp.mean(widened * widened, axis=-1, keepdims=True) + FLOOR]
    convert_element_type x0 -> x2, other arithmetic: none -> 2.08 us  [the longest x1 1.04 us: per_device(): flat.astype(F32)]
  transfers between devices with their start and end apart: 15 -> 19, of which waited for: 10 -> 11; matrix products, arithmetic and copies ran while one was open for 17% -> 11% of each run, Pallas kernels for 0% -> 0%
where the time goes in v2:
time: 163 us; the launch traced here: 162 us
  waiting for transfers between devices  43.4 us (27%)
  matrix products  38.4 us (24%)
  starting transfers between devices  29.9 us (18%)
  Pallas kernels  21.7 us (13%)
  other arithmetic  18.5 us (11%)
  local copies, waits for them, and re-layouts  9.03 us (6%)
    dot_general x8, matrix products, project(): return jnp.dot(normed, weights, preferred_element_type=F32).astype(BF)  26.1 us
    ppermute x2, waiting for transfers between devices, per_device(): lax.ppermute(value, 'tm', cyclic('tm', shift))  18.1 us
    pallas_call x2, Pallas kernels, spatial_attend(): pl.pallas_call(functools.partial(spatial_kernel, rows, cols, all_rows), g...  14.4 us
    ppermute x5, waiting for transfers between devices, scatter_rows(): arrived = lax.ppermute(take((me + shift) % n), axis, cyclic(axis, shift))  9.72 us
    ppermute x2, starting transfers between devices, per_device(): above = lax.ppermute(here[rows - HALO:], 'space', up).reshape(span, depth)  8.98 us
    ppermute x2, waiting for transfers between devices, per_device(): lax.ppermute(block, 'tm', cyclic('tm', shift))  8.84 us
    ppermute x5, starting transfers between devices, scatter_rows(): arrived = lax.ppermute(take((me + shift) % n), axis, cyclic(axis, shift))  8.01 us
    pallas_call x1, Pallas kernels, temporal_attend(): pl.pallas_call(functools.partial(temporal_kernel, frames, keys), grid=(to...  7.3 us
  transfers between devices with their start and end apart: 19, of which 11 were waited for; matrix products, arithmetic and copies ran while one was open for 11% of the time, Pallas kernels for 0%

profile of v2, /device:TPU:0, one launch (start us, length us, event | category | flops | bytes accessed | tf_op | source)
XLA Modules:
  0.0 161.9 jit_solution(5429102423735918774)
XLA Ops:
  0.7 1.2 dynamic-slice_bitcast_fusion
  1.9 3.0 %collective-permute-start = (bf16[8,16,1024]{2,1,0:T(8,128)(2,1)S(1)}, bf16[8,16,1024]{2,1,0:T(8,128)(2,1)S(1)}, u32[]{:S(2)}, u32[]{:S(2)}) collective-permute-start(bf16[8,16,1024]{2,1,0:T(8,128)(2,1)S(1)} %get-tuple-element.27), channel_id=1, source_target_pairs={{0,4},{4,0},{1,5},{5,1},{2,6},{6,2},{3,7},{7,3},{8,12},{12,8},{9,1... | collective-permute-start | bytes 786440 | tf_op jit(solution)/shard_map/ppermute | solution.py:219
  5.0 0.9 fusion.46.gather_ref
  5.9 1.3 fusion.66
  7.2 0.8 fusion.47.spread_ref
  8.0 4.1 %collective-permute-done = bf16[8,16,1024]{2,1,0:T(8,128)(2,1)S(1)} collective-permute-done((bf16[8,16,1024]{2,1,0:T(8,128)(2,1)S(1)}, bf16[8,16,1024]{2,1,0:T(8,128)(2,1)S(1)}, u32[]{:S(2)}, u32[]{:S(2)}) %collective-permute-start) | collective-permute-done | bytes 262176 | tf_op jit(solution)/shard_map/ppermute | solution.py:219
  12.1 4.8 %collective-permute-done.3 = bf16[8,16,1024]{2,1,0:T(8,128)(2,1)S(1)} collective-permute-done((bf16[8,16,1024]{2,1,0:T(8,128)(2,1)S(1)}, bf16[8,16,1024]{2,1,0:T(8,128)(2,1)S(1)}, u32[]{:S(2)}, u32[]{:S(2)}) %collective-permute-start.3) | collective-permute-done | bytes 262176 | tf_op jit(solution)/shard_map/ppermute | solution.py:219
  16.8 1.1 fusion.52
  18.2 0.9 fusion.50
  19.2 1.3 collective-permute-start.2
  20.5 5.3 %collective-permute-start.1 = (bf16[4,32,1024]{2,1,0:T(8,128)(2,1)}, bf16[4,32,1024]{2,1,0:T(8,128)(2,1)}, u32[]{:S(2)}, u32[]{:S(2)}) collective-permute-start(bf16[4,32,1024]{2,1,0:T(8,128)(2,1)} %bitcast.8), channel_id=1, source_target_pairs={{0,1},{1,2},{2,3},{4,5},{5,6},{6,7},{8,9},{9,10},{10,11},{12,13},{... | collective-permute-start | bytes 786440 | tf_op jit(solution)/shard_map/ppermute | solution.py:223
  25.8 0.7 copy.38
  26.5 3.7 %collective-permute-start.4 = (bf16[4,32,1024]{2,1,0:T(8,128)(2,1)}, bf16[4,32,1024]{2,1,0:T(8,128)(2,1)}, u32[]{:S(2)}, u32[]{:S(2)}) collective-permute-start(bf16[4,32,1024]{2,1,0:T(8,128)(2,1)} %bitcast.18), channel_id=1, source_target_pairs={{0,1},{1,2},{2,3},{4,5},{5,6},{6,7},{8,9},{9,10},{10,11},{12,13},{... | collective-permute-start | bytes 786440 | tf_op jit(solution)/shard_map/ppermute | solution.py:223
  30.2 0.7 copy.39
  31.0 1.3 collective-permute-start.5
  32.3 1.0 fusion.45
  33.3 1.0 fusion.44
  34.6 1.4 copy.36
  36.0 1.3 fusion.22
  37.3 2.2 %collective-permute-done.5 = bf16[4,32,1024]{2,1,0:T(8,128)(2,1)} collective-permute-done((bf16[4,32,1024]{2,1,0:T(8,128)(2,1)}, bf16[4,32,1024]{2,1,0:T(8,128)(2,1)}, u32[]{:S(2)}, u32[]{:S(2)}) %collective-permute-start.5) | collective-permute-done | bytes 262176 | tf_op jit(solution)/shard_map/ppermute | solution.py:224
  39.5 1.2 fusion.25
  40.8 2.3 %fusion.27 = (bf16[256,1024]{1,0:T(8,128)(2,1)}, bf16[256,1024]{1,0:T(8,128)(2,1)S(1)}, bf16[256,1024]{1,0:T(8,128)(2,1)S(1)}, bf16[256,1024]{1,0:T(8,128)(2,1)S(1)}) fusion(f32[256]{0:T(256)S(1)} %add_rsqrt_fusion.6, f32[1024]{0:T(1024)S(1)} %copy-done.6, bf16[128,1024]{1,0:T(8,128)(2,1)} %bitcast.21, bf16[128,1024]{1,0:T(8,128)(2,1)} %bitcast.19, ...), kind=kLoop, calls=%fused_computation.40 | loop fusion | flops 5242880 | bytes 5251072 | tf_op jit(solution)/shard_map/convert_element_type | solution.py:23
  43.1 3.0 %convolution_convert_fusion.3.q_ref.k_ref.v_ref = bf16[256,3072]{1,0:T(8,128)(2,1)} fusion(bf16[256,1024]{1,0:T(8,128)(2,1)S(1)} %get-tuple-element.46, bf16[1024,3072]{1,0:T(8,128)(2,1)S(1)} %copy-done.10), kind=kOutput, calls=%fused_computation.3 | convolution fusion | flops 1611399168 | bytes 8388608 | tf_op jit(solution)/shard_map/dot_general | solution.py:212
  46.1 2.3 %fusion.8.kt_ref.vt_ref.kb_ref.vb_ref = bf16[256,2048]{1,0:T(8,128)(2,1)} fusion(bf16[256,1024]{1,0:T(8,128)(2,1)S(1)} %get-tuple-element.44, bf16[1024,3072]{1,0:T(8,128)(2,1)S(1)} %copy-done.10), kind=kOutput, calls=%fused_computation.12 | convolution fusion | flops 1074266112 | bytes 5767168 | tf_op jit(solution)/shard_map/dot_general | solution.py:212
  48.3 3.0 %convolution_convert_fusion.2.q_ref.k_ref.v_ref = bf16[256,3072]{1,0:T(8,128)(2,1)} fusion(bf16[256,1024]{1,0:T(8,128)(2,1)S(1)} %get-tuple-element.45, bf16[1024,3072]{1,0:T(8,128)(2,1)S(1)} %copy-done.10), kind=kOutput, calls=%fused_computation.2 | convolution fusion | flops 1611399168 | bytes 8388608 | tf_op jit(solution)/shard_map/dot_general | solution.py:212
  51.3 7.3 %spatial.2 = bf16[256,1024]{1,0:T(8,128)(2,1)} custom-call(s32[1]{0:T(128)} %bitcast.6.reach_ref, s32[1]{0:T(128)} %bitcast.7.first_ref, bf16[256,3072]{1,0:T(8,128)(2,1)} %convolution_convert_fusion.3.q_ref.k_ref.v_ref, bf16[256,3072]{1,0:T(8,128)(2,1)} %convolution_convert_fusion.3.q_ref.k_ref.v_ref, ...), custom_call_target="tpu_custom_call" | custom-call | flops 805306368 | bytes 3145728 | tf_op jit(solution)/shard_map/spatial/pallas_call | solution.py:79
  58.7 3.0 %fusion.20 = bf16[256,1024]{1,0:T(8,128)(2,1)} fusion(f32[256,1024]{1,0:T(8,128)} %bitcast.79, bf16[256,1024]{1,0:T(8,128)(2,1)} %spatial.2, bf16[1024,1024]{1,0:T(8,128)(2,1)S(1)} %copy-done), kind=kOutput, calls=%fused_computation.33 | convolution fusion | flops 537395200 | bytes 4194304 | tf_op jit(solution)/shard_map/dot_general | solution.py:234
  61.6 4.4 %fusion.11.kt_ref.vt_ref.kb_ref.vb_ref = bf16[256,2048]{1,0:T(8,128)(2,1)} fusion(bf16[256,1024]{1,0:T(8,128)(2,1)S(1)} %copy-done.5, bf16[1024,3072]{1,0:T(8,128)(2,1)} %param.14), kind=kOutput, calls=%fused_computation.13 | convolution fusion | flops 1074266112 | bytes 5767168 | tf_op jit(solution)/shard_map/dot_general | solution.py:212
  66.0 7.1 %spatial.3 = bf16[256,1024]{1,0:T(8,128)(2,1)} custom-call(s32[1]{0:T(128)} %bitcast.17.reach_ref, s32[1]{0:T(128)} %bitcast.7.first_ref, bf16[256,3072]{1,0:T(8,128)(2,1)} %convolution_convert_fusion.2.q_ref.k_ref.v_ref, bf16[256,3072]{1,0:T(8,128)(2,1)} %convolution_convert_fusion.2.q_ref.k_ref.v_ref, ...), custom_call_target="tpu_custom_call" | custom-call | flops 805306368 | bytes 3145728 | tf_op jit(solution)/shard_map/spatial/pallas_call | solution.py:79
  73.1 2.6 %fusion.31 = (f32[256]{0:T(256)S(1)}, bf16[256,1024]{1,0:T(8,128)(2,1)}) fusion(f32[256,1024]{1,0:T(8,128)S(1)} %bitcast.78, bf16[256,1024]{1,0:T(8,128)(2,1)} %spatial.3, bf16[1024,1024]{1,0:T(8,128)(2,1)S(1)} %copy-done), kind=kOutput, calls=%fused_computation.44 | convolution fusion | flops 538181376 | bytes 4195328 | tf_op jit(solution)/shard_map/dot_general | solution.py:234
  75.7 1.5 collective-permute-start.7
  77.3 0.7 pad_add_fusion.k_order
  77.9 0.5 collective-permute-start.6
  78.5 1.3 fusion.28
  79.7 11.0 %collective-permute-done.7 = bf16[256,1024]{1,0:T(8,128)(2,1)S(1)} collective-permute-done((bf16[256,1024]{1,0:T(8,128)(2,1)}, bf16[256,1024]{1,0:T(8,128)(2,1)S(1)}, u32[]{:S(2)}, u32[]{:S(2)}) %collective-permute-start.7) | collective-permute-done | bytes 524320 | tf_op jit(solution)/shard_map/ppermute | solution.py:238
  90.9 7.1 %collective-permute-done.6 = bf16[256,1024]{1,0:T(8,128)(2,1)S(1)} collective-permute-done((bf16[256,1024]{1,0:T(8,128)(2,1)}, bf16[256,1024]{1,0:T(8,128)(2,1)S(1)}, u32[]{:S(2)}, u32[]{:S(2)}) %collective-permute-start.6) | collective-permute-done | bytes 524320 | tf_op jit(solution)/shard_map/ppermute | solution.py:238
  98.2 1.9 %fusion.39 = (bf16[256,1024]{1,0:T(8,128)(2,1)S(1)}, bf16[256,1024]{1,0:T(8,128)(2,1)S(1)}, bf16[256,1024]{1,0:T(8,128)(2,1)S(1)}, bf16[256,1024]{1,0:T(8,128)(2,1)S(1)}) fusion(bf16[256,1024]{1,0:T(8,128)(2,1)S(1)} %collective-permute-done.7, f32[256]{0:T(256)S(1)} %add_rsqrt_fusion.2, f32[1024]{0:T(1024)S(1)} %copy-done.7, f32[256]{0:T(256)S(1)} %get-tuple-element.53, ...), kind=kLoop, calls=%fused_computation.52 | loop fusion | flops 4194304 | bytes 4202496 | tf_op jit(solution)/shard_map/convert_element_type | solution.py:23
  100.1 5.9 %convolution_convert_fusion.refs_1_.refs_3_.refs_7_ = bf16[256,3072]{1,0:T(8,128)(2,1)} fusion(bf16[256,1024]{1,0:T(8,128)(2,1)S(1)} %get-tuple-element.40, bf16[1024,3072]{1,0:T(8,128)(2,1)} %param.17), kind=kOutput, calls=%fused_computation | convolution fusion | flops 1611399168 | bytes 8388608 | tf_op jit(solution)/shard_map/dot_general | solution.py:212
  106.0 3.0 %convolution_convert_fusion.1.refs_0_.refs_2_.refs_6_ = bf16[256,3072]{1,0:T(8,128)(2,1)} fusion(bf16[256,1024]{1,0:T(8,128)(2,1)S(1)} %get-tuple-element.42, bf16[1024,3072]{1,0:T(8,128)(2,1)S(1)} %bitcast.85), kind=kOutput, calls=%fused_computation.1 | convolution fusion | flops 1611399168 | bytes 8388608 | tf_op jit(solution)/shard_map/dot_general | solution.py:212
  109.0 2.2 %fusion.14.refs_4_.refs_8_ = bf16[256,2048]{1,0:T(8,128)(2,1)} fusion(bf16[256,1024]{1,0:T(8,128)(2,1)S(1)} %get-tuple-element.41, bf16[1024,3072]{1,0:T(8,128)(2,1)S(1)} %bitcast.85), kind=kOutput, calls=%fused_computation.14 | convolution fusion | flops 1074266112 | bytes 5767168 | tf_op jit(solution)/shard_map/dot_general | solution.py:212
  111.3 2.3 %fusion.17.refs_5_.refs_9_ = bf16[256,2048]{1,0:T(8,128)(2,1)} fusion(bf16[256,1024]{1,0:T(8,128)(2,1)S(1)} %get-tuple-element.39, bf16[1024,3072]{1,0:T(8,128)(2,1)S(1)} %bitcast.85), kind=kOutput, calls=%fused_computation.15 | convolution fusion | flops 1074266112 | bytes 5767168 | tf_op jit(solution)/shard_map/dot_general | solution.py:212
  113.6 7.3 %temporal.1 = bf16[2,256,1024]{2,1,0:T(8,128)(2,1)} custom-call(s32[2]{0:T(128)} %copy-done.8, s32[4]{0:T(128)} %pad_add_fusion.k_order, bf16[1024,128]{1,0:T(8,128)(2,1)} %fusion.46.gather_ref, bf16[128,1024]{1,0:T(8,128)(2,1)} %fusion.47.spread_ref, bf16[256,3072]{1,0:T(8,128)(2,1)} %convolution_convert_fusion.1.refs_0_.refs_2_.refs_6_, ...), custom_call_target="tpu_custom_call" | custom-call | flops 1073741824 | bytes 4194304 | tf_op jit(solution)/shard_map/temporal/pallas_call | solution.py:124
  120.9 2.5 %convolution_convert_fusion.4 = bf16[1024,1024]{0,1:T(8,128)(2,1)S(1)} fusion(bf16[512,1024]{1,0:T(8,128)(2,1)} %bitcast.82, bf16[512,1024]{1,0:T(8,128)(2,1)S(1)} %bitcast.86), kind=kOutput, calls=%fused_computation.18 | convolution fusion | flops 1074790400 | bytes 4194304 | tf_op jit(solution)/shard_map/dot_general | solution.py:243
  123.4 1.3 copy-done.3
  124.9 2.8 %collective-permute-done.8 = bf16[1024,512]{0,1:T(8,128)(2,1)} collective-permute-done((bf16[1024,512]{0,1:T(8,128)(2,1)S(1)}, bf16[1024,512]{0,1:T(8,128)(2,1)}, u32[]{:S(2)}, u32[]{:S(2)}) %collective-permute-start.8) | collective-permute-done | bytes 1048608 | tf_op jit(solution)/shard_map/ppermute | solution.py:145
  127.7 1.9 %add_convert_fusion = bf16[1024,512]{0,1:T(8,128)(2,1)S(1)} fusion(bf16[1024,512]{0,1:T(8,128)(2,1)} %collective-permute-done.8, bf16[1024,1024]{0,1:T(8,128)(2,1)} %copy-done.3, s32[]{:T(128)S(6)} %select_n.265), kind=kLoop, calls=%fused_computation.16 | loop fusion | flops 2097152 | bytes 3145732 | tf_op jit(solution)/shard_map/convert_element_type | solution.py:154
  129.7 0.8 copy-done.4
  130.5 1.6 collective-permute-start.11
  132.1 1.6 collective-permute-start.9
  133.7 5.3 %collective-permute-done.11 = bf16[512,256]{0,1:T(8,128)(2,1)} collective-permute-done((bf16[512,256]{0,1:T(8,128)(2,1)S(1)}, bf16[512,256]{0,1:T(8,128)(2,1)}, u32[]{:S(2)}, u32[]{:S(2)}) %collective-permute-start.11) | collective-permute-done | bytes 262176 | tf_op jit(solution)/shard_map/ppermute | solution.py:163
  139.0 1.1 add_convert_fusion.2
  140.1 1.6 collective-permute-start.12
  141.8 1.6 collective-permute-start.10
  143.4 1.8 %collective-permute-done.12 = bf16[512,128]{0,1:T(8,128)(2,1)S(1)} collective-permute-done((bf16[512,128]{0,1:T(8,128)(2,1)S(1)}, bf16[512,128]{0,1:T(8,128)(2,1)S(1)}, u32[]{:S(2)}, u32[]{:S(2)}) %collective-permute-start.12) | collective-permute-done | bytes 131104 | tf_op jit(solution)/shard_map/ppermute | solution.py:145
  145.2 1.6 %collective-permute-done.10 = bf16[512,128]{0,1:T(8,128)(2,1)S(1)} collective-permute-done((bf16[512,128]{0,1:T(8,128)(2,1)S(1)}, bf16[512,128]{0,1:T(8,128)(2,1)S(1)}, u32[]{:S(2)}, u32[]{:S(2)}) %collective-permute-start.10) | collective-permute-done | bytes 131104 | tf_op jit(solution)/shard_map/ppermute | solution.py:163
  147.0 1.6 %collective-permute-start.13 = (bf16[128,256]{0,1:T(8,128)(2,1)S(1)}, bf16[128,256]{0,1:T(8,128)(2,1)S(1)}, u32[]{:S(2)}, u32[]{:S(2)}) collective-permute-start(bf16[128,256]{0,1:T(8,128)(2,1)S(1)} %get-tuple-element.36), channel_id=1, source_target_pairs={{0,1},{1,2},{2,3},{3,0},{4,5},{5,6},{6,7},{7,4},{8,9},{9,10},{10,1... | collective-permute-start | bytes 196616 | tf_op jit(solution)/shard_map/ppermute | solution.py:163
  148.6 1.3 collective-permute-start.14
  149.9 1.9 %collective-permute-start.15 = (bf16[128,256]{0,1:T(8,128)(2,1)S(1)}, bf16[128,256]{0,1:T(8,128)(2,1)S(1)}, u32[]{:S(2)}, u32[]{:S(2)}) collective-permute-start(bf16[128,256]{0,1:T(8,128)(2,1)S(1)} %get-tuple-element.38), channel_id=1, source_target_pairs={{0,3},{1,0},{2,1},{3,2},{4,7},{5,4},{6,5},{7,6},{8,11},{9,8},{10,9... | collective-permute-start | bytes 196616 | tf_op jit(solution)/shard_map/ppermute | solution.py:163
  151.9 1.2 collective-permute-done.13
  153.1 1.5 collective-permute-done.14
  154.7 0.6 collective-permute-start.17
  155.3 1.3 collective-permute-start.18
  156.6 4.2 %add_convert_fusion.1 = bf16[512,1024]{1,0:T(8,128)(2,1)} fusion(bf16[512,1024]{1,0:T(8,128)(2,1)} %bitcast.83, bf16[1024,1024]{1,0:T(8,128)(2,1)} %param.18, bf16[256,1024]{1,0:T(8,128)(2,1)} %get-tuple-element.52, bf16[256,1024]{1,0:T(8,128)(2,1)S(1)} %copy-done.2), kind=kOutput, calls=%fused_computation.17 | convolution fusion | flops 1076887552 | bytes 5242880 | tf_op jit(solution)/shard_map/dot_general | solution.py:246
  160.9 0.9 copy.40
  (75 shorter events, 2.0 us)
Async XLA Ops:
  0.6 58.0 %copy-start = (bf16[1024,1024]{1,0:T(8,128)(2,1)S(1)}, bf16[1024,1024]{1,0:T(8,128)(2,1)}, u32[]{:S(2)}) copy-start(bf16[1024,1024]{1,0:T(8,128)(2,1)} %param.15) | copy-start | bytes 6291460
  1.9 10.2 %collective-permute-start = (bf16[8,16,1024]{2,1,0:T(8,128)(2,1)S(1)}, bf16[8,16,1024]{2,1,0:T(8,128)(2,1)S(1)}, u32[]{:S(2)}, u32[]{:S(2)}) collective-permute-start(bf16[8,16,1024]{2,1,0:T(8,128)(2,1)S(1)} %get-tuple-element.27), channel_id=1, source_target_pairs={{0,4},{4,0},{1,5},{5,1},{2,6},{6,2},{3,7},{7,3},{8,12},{12,8},{9,1... | collective-permute-start | bytes 786440 | tf_op jit(solution)/shard_map/ppermute | solution.py:219
  4.9 11.9 %collective-permute-start.3 = (bf16[8,16,1024]{2,1,0:T(8,128)(2,1)S(1)}, bf16[8,16,1024]{2,1,0:T(8,128)(2,1)S(1)}, u32[]{:S(2)}, u32[]{:S(2)}) collective-permute-start(bf16[8,16,1024]{2,1,0:T(8,128)(2,1)S(1)} %get-tuple-element.26), channel_id=1, source_target_pairs={{0,4},{4,0},{1,5},{5,1},{2,6},{6,2},{3,7},{7,3},{8,12},{12,8},{9,1... | collective-permute-start | bytes 786440 | tf_op jit(solution)/shard_map/ppermute | solution.py:219
  19.2 16.7 %collective-permute-start.2 = (bf16[4,32,1024]{2,1,0:T(8,128)(2,1)}, bf16[4,32,1024]{2,1,0:T(8,128)(2,1)S(1)}, u32[]{:S(2)}, u32[]{:S(2)}) collective-permute-start(bf16[4,32,1024]{2,1,0:T(8,128)(2,1)} %bitcast.10), channel_id=1, source_target_pairs={{1,0},{2,1},{3,2},{5,4},{6,5},{7,6},{9,8},{10,9},{11,10},{13,12},{... | collective-permute-start | bytes 786440 | tf_op jit(solution)/shard_map/ppermute | solution.py:224
  20.5 15.4 %collective-permute-start.1 = (bf16[4,32,1024]{2,1,0:T(8,128)(2,1)}, bf16[4,32,1024]{2,1,0:T(8,128)(2,1)}, u32[]{:S(2)}, u32[]{:S(2)}) collective-permute-start(bf16[4,32,1024]{2,1,0:T(8,128)(2,1)} %bitcast.8), channel_id=1, source_target_pairs={{0,1},{1,2},{2,3},{4,5},{5,6},{6,7},{8,9},{9,10},{10,11},{12,13},{... | collective-permute-start | bytes 786440 | tf_op jit(solution)/shard_map/ppermute | solution.py:223
  26.5 10.7 %collective-permute-start.4 = (bf16[4,32,1024]{2,1,0:T(8,128)(2,1)}, bf16[4,32,1024]{2,1,0:T(8,128)(2,1)}, u32[]{:S(2)}, u32[]{:S(2)}) collective-permute-start(bf16[4,32,1024]{2,1,0:T(8,128)(2,1)} %bitcast.18), channel_id=1, source_target_pairs={{0,1},{1,2},{2,3},{4,5},{5,6},{6,7},{8,9},{9,10},{10,11},{12,13},{... | collective-permute-start | bytes 786440 | tf_op jit(solution)/shard_map/ppermute | solution.py:223
  31.0 8.6 %collective-permute-start.5 = (bf16[4,32,1024]{2,1,0:T(8,128)(2,1)}, bf16[4,32,1024]{2,1,0:T(8,128)(2,1)}, u32[]{:S(2)}, u32[]{:S(2)}) collective-permute-start(bf16[4,32,1024]{2,1,0:T(8,128)(2,1)} %bitcast.20), channel_id=1, source_target_pairs={{1,0},{2,1},{3,2},{5,4},{6,5},{7,6},{9,8},{10,9},{11,10},{13,12},{... | collective-permute-start | bytes 786440 | tf_op jit(solution)/shard_map/ppermute | solution.py:224
  33.3 7.4 %copy-start.6 = (f32[1024]{0:T(1024)S(1)}, f32[1024]{0:T(1024)}, u32[]{:S(2)}) copy-start(f32[1024]{0:T(1024)} %param.13) | copy-start | bytes 12292
  34.6 6.2 %copy-start.1 = (f32[8,2,16,1024]{3,2,1,0:T(8,128)S(1)}, f32[8,2,16,1024]{3,2,1,0:T(8,128)}, u32[]{:S(2)}) copy-start(f32[8,2,16,1024]{3,2,1,0:T(8,128)} %fusion.45) | copy-start | bytes 3145732
  36.0 7.1 %copy-start.10 = (bf16[1024,3072]{1,0:T(8,128)(2,1)S(1)}, bf16[1024,3072]{1,0:T(8,128)(2,1)}, u32[]{:S(2)}) copy-start(bf16[1024,3072]{1,0:T(8,128)(2,1)} %param.14) | copy-start | bytes 18874372
  58.7 3.0 %copy-start.5 = (bf16[256,1024]{1,0:T(8,128)(2,1)S(1)}, bf16[256,1024]{1,0:T(8,128)(2,1)}, u32[]{:S(2)}) copy-start(bf16[256,1024]{1,0:T(8,128)(2,1)} %get-tuple-element.43) | copy-start | bytes 1572868
  73.1 4.1 %copy-start.9 = (s32[1,4]{1,0:T(1,128)S(1)}, s32[1,4]{1,0:T(1,128)}, u32[]{:S(2)}) copy-start(s32[1,4]{1,0:T(1,128)} %param.11) | copy-start | bytes 52
  73.1 25.1 %copy-start.7 = (f32[1024]{0:T(1024)S(1)}, f32[1024]{0:T(1024)}, u32[]{:S(2)}) copy-start(f32[1024]{0:T(1024)} %param.16) | copy-start | bytes 12292
  75.7 15.0 %collective-permute-start.7 = (bf16[256,1024]{1,0:T(8,128)(2,1)}, bf16[256,1024]{1,0:T(8,128)(2,1)S(1)}, u32[]{:S(2)}, u32[]{:S(2)}) collective-permute-start(bf16[256,1024]{1,0:T(8,128)(2,1)} %get-tuple-element.52), channel_id=1, source_target_pairs={{0,4},{4,0},{1,5},{5,1},{2,6},{6,2},{3,7},{7,3},{8,12},{12,8},{9,1... | collective-permute-start | bytes 1572872 | tf_op jit(solution)/shard_map/ppermute | solution.py:238
  77.3 22.8 %copy-start.8 = (s32[2]{0:T(128)}, s32[2]{0:T(128)S(1)}, u32[]{:S(2)}) copy-start(s32[2]{0:T(128)S(1)} %get-tuple-element.50.q_order) | copy-start | bytes 28
  77.9 20.0 %collective-permute-start.6 = (bf16[256,1024]{1,0:T(8,128)(2,1)}, bf16[256,1024]{1,0:T(8,128)(2,1)S(1)}, u32[]{:S(2)}, u32[]{:S(2)}) collective-permute-start(bf16[256,1024]{1,0:T(8,128)(2,1)} %fusion.20), channel_id=1, source_target_pairs={{0,4},{4,0},{1,5},{5,1},{2,6},{6,2},{3,7},{7,3},{8,12},{12,8},{9,1... | collective-permute-start | bytes 1572872 | tf_op jit(solution)/shard_map/ppermute | solution.py:238
  98.2 7.8 %slice-start = ((s8[6291456]{0:T(1024)(128)(4,1)}), s8[4194304]{0:T(1024)(128)(4,1)S(1)}, s32[]{:S(2)}) async-start(s8[6291456]{0:T(1024)(128)(4,1)} %bitcast.84), calls=%async_computation | async-start | bytes 8388608
  100.1 5.9 %slice-start.1 = ((s8[6291456]{0:T(1024)(128)(4,1)}), s8[2097152]{0:T(1024)(128)(4,1)S(1)}, s32[]{:S(2)}) async-start(s8[6291456]{0:T(1024)(128)(4,1)} %bitcast.84), calls=%async_computation.1 | async-start | bytes 4194304
  113.6 7.3 %copy-start.11 = (bf16[1,2,8,32,1024]{4,3,2,1,0:T(8,128)(2,1)S(1)}, bf16[1,2,8,32,1024]{4,3,2,1,0:T(8,128)(2,1)}, u32[]{:S(2)}) copy-start(bf16[1,2,8,32,1024]{4,3,2,1,0:T(8,128)(2,1)} %param.19) | copy-start | bytes 3145732
  123.4 1.3 copy-start.3
  124.8 2.9 %collective-permute-start.8 = (bf16[1024,512]{0,1:T(8,128)(2,1)S(1)}, bf16[1024,512]{0,1:T(8,128)(2,1)}, u32[]{:S(2)}, u32[]{:S(2)}) collective-permute-start(bf16[1024,512]{0,1:T(8,128)(2,1)S(1)} %constant_dynamic-slice_fusion.4), channel_id=1, source_target_pairs={{0,8},{8,0},{16,24},{24,16},{1,9},{9,1},{17,25},{25,17},{2,10},{10... | collective-permute-start | bytes 3145736 | tf_op jit(solution)/shard_map/ppermute | solution.py:145
  129.7 0.8 copy-start.4
  130.5 8.5 %collective-permute-start.11 = (bf16[512,256]{0,1:T(8,128)(2,1)S(1)}, bf16[512,256]{0,1:T(8,128)(2,1)}, u32[]{:S(2)}, u32[]{:S(2)}) collective-permute-start(bf16[512,256]{0,1:T(8,128)(2,1)S(1)} %constant_dynamic-slice_fusion.1), channel_id=1, source_target_pairs={{0,4},{4,0},{1,5},{5,1},{2,6},{6,2},{3,7},{7,3},{8,12},{12,8},{9,1... | collective-permute-start | bytes 786440 | tf_op jit(solution)/shard_map/ppermute | solution.py:163
  132.1 24.5 %copy-start.2 = (bf16[256,1024]{1,0:T(8,128)(2,1)S(1)}, bf16[256,1024]{1,0:T(8,128)(2,1)}, u32[]{:S(2)}) copy-start(bf16[256,1024]{1,0:T(8,128)(2,1)} %fusion.20) | copy-start | bytes 1572868
  132.1 9.7 %collective-permute-start.9 = (bf16[1024,128]{0,1:T(8,128)(2,1)S(1)}, bf16[1024,128]{0,1:T(8,128)(2,1)S(1)}, u32[]{:S(2)}, u32[]{:S(2)}) collective-permute-start(bf16[1024,128]{0,1:T(8,128)(2,1)S(1)} %constant_dynamic-slice_fusion.3), channel_id=1, source_target_pairs={{0,16},{8,24},{16,0},{24,8},{1,17},{9,25},{17,1},{25,9},{2,18},{10... | collective-permute-start | bytes 786440 | tf_op jit(solution)/shard_map/ppermute | solution.py:145
  140.1 5.0 %collective-permute-start.12 = (bf16[512,128]{0,1:T(8,128)(2,1)S(1)}, bf16[512,128]{0,1:T(8,128)(2,1)S(1)}, u32[]{:S(2)}, u32[]{:S(2)}) collective-permute-start(bf16[512,128]{0,1:T(8,128)(2,1)S(1)} %constant_dynamic-slice_fusion), channel_id=1, source_target_pairs={{0,16},{8,24},{16,0},{24,8},{1,17},{9,25},{17,1},{25,9},{2,18},{10... | collective-permute-start | bytes 393224 | tf_op jit(solution)/shard_map/ppermute | solution.py:145
  141.8 5.0 %collective-permute-start.10 = (bf16[512,128]{0,1:T(8,128)(2,1)S(1)}, bf16[512,128]{0,1:T(8,128)(2,1)S(1)}, u32[]{:S(2)}, u32[]{:S(2)}) collective-permute-start(bf16[512,128]{0,1:T(8,128)(2,1)S(1)} %constant_dynamic-slice_fusion.2), channel_id=1, source_target_pairs={{0,4},{4,0},{1,5},{5,1},{2,6},{6,2},{3,7},{7,3},{8,12},{12,8},{9,1... | collective-permute-start | bytes 393224 | tf_op jit(solution)/shard_map/ppermute | solution.py:163
  147.0 6.1 %collective-permute-start.13 = (bf16[128,256]{0,1:T(8,128)(2,1)S(1)}, bf16[128,256]{0,1:T(8,128)(2,1)S(1)}, u32[]{:S(2)}, u32[]{:S(2)}) collective-permute-start(bf16[128,256]{0,1:T(8,128)(2,1)S(1)} %get-tuple-element.36), channel_id=1, source_target_pairs={{0,1},{1,2},{2,3},{3,0},{4,5},{5,6},{6,7},{7,4},{8,9},{9,10},{10,1... | collective-permute-start | bytes 196616 | tf_op jit(solution)/shard_map/ppermute | solution.py:163
  148.6 6.0 %collective-permute-start.14 = (bf16[128,256]{0,1:T(8,128)(2,1)S(1)}, bf16[128,256]{0,1:T(8,128)(2,1)S(1)}, u32[]{:S(2)}, u32[]{:S(2)}) collective-permute-start(bf16[128,256]{0,1:T(8,128)(2,1)S(1)} %get-tuple-element.37), channel_id=1, source_target_pairs={{0,2},{1,3},{2,0},{3,1},{4,6},{5,7},{6,4},{7,5},{8,10},{9,11},{10,... | collective-permute-start | bytes 196616 | tf_op jit(solution)/shard_map/ppermute | solution.py:163
  149.9 4.7 %collective-permute-start.15 = (bf16[128,256]{0,1:T(8,128)(2,1)S(1)}, bf16[128,256]{0,1:T(8,128)(2,1)S(1)}, u32[]{:S(2)}, u32[]{:S(2)}) collective-permute-start(bf16[128,256]{0,1:T(8,128)(2,1)S(1)} %get-tuple-element.38), channel_id=1, source_target_pairs={{0,3},{1,0},{2,1},{3,2},{4,7},{5,4},{6,5},{7,6},{8,11},{9,8},{10,9... | collective-permute-start | bytes 196616 | tf_op jit(solution)/shard_map/ppermute | solution.py:163
  154.6 6.1 %collective-permute-start.16 = (bf16[128,256]{0,1:T(8,128)(2,1)S(1)}, bf16[128,256]{0,1:T(8,128)(2,1)S(1)}, u32[]{:S(2)}, u32[]{:S(2)}) collective-permute-start(bf16[128,256]{0,1:T(8,128)(2,1)S(1)} %add_convert_fusion.6), channel_id=1, source_target_pairs={{0,8},{8,0},{16,24},{24,16},{1,9},{9,1},{17,25},{25,17},{2,10},{10... | collective-permute-start | bytes 196616 | tf_op jit(solution)/shard_map/ppermute | solution.py:145
  154.7 6.1 %collective-permute-start.17 = (bf16[128,256]{0,1:T(8,128)(2,1)S(1)}, bf16[128,256]{0,1:T(8,128)(2,1)S(1)}, u32[]{:S(2)}, u32[]{:S(2)}) collective-permute-start(bf16[128,256]{0,1:T(8,128)(2,1)S(1)} %add_convert_fusion.6), channel_id=1, source_target_pairs={{0,16},{8,24},{16,0},{24,8},{1,17},{9,25},{17,1},{25,9},{2,18},{10... | collective-permute-start | bytes 196616 | tf_op jit(solution)/shard_map/ppermute | solution.py:145
  155.3 5.5 %collective-permute-start.18 = (bf16[128,256]{0,1:T(8,128)(2,1)S(1)}, bf16[128,256]{0,1:T(8,128)(2,1)S(1)}, u32[]{:S(2)}, u32[]{:S(2)}) collective-permute-start(bf16[128,256]{0,1:T(8,128)(2,1)S(1)} %add_convert_fusion.6), channel_id=1, source_target_pairs={{0,24},{8,16},{16,8},{24,0},{1,25},{9,17},{17,9},{25,1},{2,26},{10... | collective-permute-start | bytes 196616 | tf_op jit(solution)/shard_map/ppermute | solution.py:145

commit v3 on v2

--- a/solution.py
+++ b/solution.py
@@ -66,20 +66,20 @@
             o_ref[here, at] = jnp.where(lane < HEAD_DIM, o[:span], o[span:]).astype(BF)
 
 
-def spatial_attend(projected, halo, reach, first_row, frames, rows, cols, all_rows):
+def spatial_attend(projected, halo, reach, first_row, frame, frames, rows, cols, all_rows):
     depth = projected.shape[1] // 3
     tokens, span = rows * cols, HALO * cols
     width = 2 * LANES
     blocks = depth // width
-    here = lambda part: pl.BlockSpec((tokens, width), lambda f, j: (f, part * blocks + j))
+    here = lambda part: pl.BlockSpec((tokens, width), lambda f, j: (frame + f, part * blocks + j))
     beside = lambda side, part: pl.BlockSpec(
-        (span, width), lambda f, j: (side * frames + f, part * blocks + j))
+        (span, width), lambda f, j: (side * frames + frame + f, part * blocks + j))
     smem = pl.BlockSpec(memory_space=pltpu.SMEM)
-    pairs = frames * HEADS * tokens * 3 * span
+    pairs = HEADS * tokens * 3 * span
     return pl.pallas_call(
         functools.partial(spatial_kernel, rows, cols, all_rows),
-        grid=(frames, blocks),
-        out_shape=jax.ShapeDtypeStruct((frames * tokens, depth), BF),
+        grid=(1, blocks),
+        out_shape=jax.ShapeDtypeStruct((tokens, depth), BF),
         in_specs=[smem, smem, here(0), here(1), here(2), beside(0, 0), beside(0, 1), beside(1, 0), beside(1, 1)],
         out_specs=pl.BlockSpec((tokens, width), lambda f, j: (f, j)),
         scratch_shapes=[
@@ -87,7 +87,7 @@
             pltpu.VMEM((tokens + 2 * span, width), BF),
             pltpu.VMEM((rows // HALO, span, 3 * span), F32),
         ],
-        cost_estimate=pl.CostEstimate(flops=4 * pairs * LANES, bytes_accessed=frames * tokens * depth * 12,
+        cost_estimate=pl.CostEstimate(flops=48 * pairs * LANES, bytes_accessed=tokens * depth * 12,
                                       transcendentals=pairs),
         name="spatial",
     )(reach, first_row, projected, projected, projected, halo, halo, halo, halo)
@@ -208,30 +208,28 @@
     reach = row_reach.reshape(-1)
 
     def project(values, gain, weights):
-        normed = lax.optimization_barrier(normalize(values, gain))
-        return jnp.dot(normed, weights, preferred_element_type=F32).astype(BF)
-
-    staged = []
+        return jnp.dot(normalize(values, gain), weights, preferred_element_type=F32).astype(BF)
+
+    pieces = []
+    for shift in range(ranks):
+        block = lax.dynamic_slice_in_dim(clip, (me + shift) % ranks * frames, frames, 0)
+        pieces.append(lax.ppermute(block, "tm", cyclic("tm", shift)) if shift else block)
+    here = jnp.stack([lax.select_n((me - j) % ranks, *pieces) if ranks > 2 else
+                      jnp.where(me == j, pieces[0], pieces[1]) for j in range(ranks)], axis=2)
+    here = here.reshape(frames, rows, cols, depth)
+    above = lax.ppermute(here[:, rows - HALO:], "space", up).reshape(frames * span, depth)
+    below = lax.ppermute(here[:, :HALO], "space", down).reshape(frames * span, depth)
+    flat = here.reshape(frames * tokens, depth)
+    projected = project(flat, spatial_gain, spatial_heads)
+    halo = project(jnp.concatenate([above, below]), spatial_gain, spatial_heads[:, depth:])
+    middles = []
     for f in range(frames):
-        pieces = []
-        for shift in range(ranks):
-            block = lax.dynamic_index_in_dim(clip, (me + shift) % ranks * frames + f, 0, keepdims=False)
-            pieces.append(lax.ppermute(block, "tm", cyclic("tm", shift)) if shift else block)
-        here = jnp.stack([lax.select_n((me - j) % ranks, *pieces) if ranks > 2 else
-                          jnp.where(me == j, pieces[0], pieces[1]) for j in range(ranks)], axis=1)
-        here = here.reshape(rows, cols, depth)
-        above = lax.ppermute(here[rows - HALO:], "space", up).reshape(span, depth)
-        below = lax.ppermute(here[:HALO], "space", down).reshape(span, depth)
-        flat = here.reshape(tokens, depth)
-        projected = project(flat, spatial_gain, spatial_heads)
-        halo = project(jnp.concatenate([above, below]), spatial_gain, spatial_heads[:, depth:])
-        staged.append((flat, projected, halo))
-    middles = []
-    for f, (flat, projected, halo) in enumerate(staged):
+        reach_now = reach[f:f + 1]
         if f:
-            middles[-1], projected = lax.optimization_barrier((middles[-1], projected))
-        context = spatial_attend(projected, halo, reach[f:f + 1], first_row, 1, rows, cols, rows * places)
-        middles.append((flat.astype(F32) + jnp.dot(context, spatial_merge, preferred_element_type=F32)).astype(BF))
+            middles[-1], reach_now = lax.optimization_barrier((middles[-1], reach_now))
+        context = spatial_attend(projected, halo, reach_now, first_row, f, frames, rows, cols, rows * places)
+        middles.append((flat[f * tokens:(f + 1) * tokens].astype(F32)
+                        + jnp.dot(context, spatial_merge, preferred_element_type=F32)).astype(BF))
 
     order = frame_order.reshape(-1)
     orders = [lax.dynamic_slice_in_dim(order, (me - shift) % ranks * frames, frames, 0) for shift in range(ranks)]

time: 163 us -> 132 us (0.81)
  waiting for transfers between devices: 43.4 us -> 29.4 us
  other arithmetic: 18.5 us -> 10.7 us
  starting transfers between devices: 29.9 us -> 24 us
  local copies, waits for them, and re-layouts: 9.03 us -> 7.15 us
    ppermute x2, waiting for transfers between devices: 18.1 us -> 2.28 us  [per_device(): lax.ppermute(value, 'tm', cyclic('tm', shift))]
    ppermute x4 -> x2, starting transfers between devices: 11.5 us -> 5.79 us  [the longest x1 4.51 us: per_device(): lax.ppermute(here[:, rows - HALO:], 'space', up)]
    convert_element_type x2 -> x1, other arithmetic: 4.21 us -> 0.31 us  [normalize(): return (scaled * gain_vector).astype(BF)]
    ppermute x4 -> x2, waiting for transfers between devices: 2.26 us -> 5.26 us  [the longest x1 4.89 us: per_device(): lax.ppermute(here[:, :HALO], 'space', down).reshape(frames * span, depth)]
    reduce_sum x7 -> x5, other arithmetic: 4.48 us -> 2.31 us  [normalize(): jnp.mean(widened * widened, axis=-1, keepdims=True) + FLOOR]
    convert_element_type x2 -> x0, other arithmetic: 2.08 us -> none  [the longest x1 1.04 us: per_device(): flat.astype(F32)]
    dot_general x2, matrix products: 5.56 us -> 3.92 us  [per_device(): jnp.dot(context, spatial_merge, preferred_element_type=F32)]
    ppermute x2 -> x1, waiting for transfers between devices: 8.84 us -> 7.59 us  [per_device(): lax.ppermute(block, 'tm', cyclic('tm', shift))]
  transfers between devices with their start and end apart: 19 -> 16, of which waited for: 11 -> 10; matrix products, arithmetic and copies ran while one was open for 11% -> 23% of each run, Pallas kernels for 0% -> 5%
where the time goes in v3:
time: 132 us; the launch traced here: 131 us
  matrix products  37.3 us (28%)
  waiting for transfers between devices  29.4 us (22%)
  starting transfers between devices  24 us (18%)
  Pallas kernels  21.5 us (16%)
  other arithmetic  10.7 us (8%)
  local copies, waits for them, and re-layouts  7.15 us (5%)
    dot_general x6, matrix products, project(): jnp.dot(normalize(values, gain), weights, preferred_element_type=F32)  26.5 us
    pallas_call x2, Pallas kernels, spatial_attend(): pl.pallas_call(functools.partial(spatial_kernel, rows, cols, all_rows), g...  14.2 us
    ppermute x5, waiting for transfers between devices, scatter_rows(): arrived = lax.ppermute(take((me + shift) % n), axis, cyclic(axis, shift))  9.68 us
    ppermute x5, starting transfers between devices, scatter_rows(): arrived = lax.ppermute(take((me + shift) % n), axis, cyclic(axis, shift))  7.88 us
    ppermute x1, waiting for transfers between devices, per_device(): lax.ppermute(block, 'tm', cyclic('tm', shift))  7.59 us
    pallas_call x1, Pallas kernels, temporal_attend(): pl.pallas_call(functools.partial(temporal_kernel, frames, keys), grid=(to...  7.3 us
    ppermute x6, starting transfers between devices, exchange_bit(): return lax.ppermute(value, axis, [(i, i ^ bit) for i in range(n)])  5.17 us
    ppermute x1, waiting for transfers between devices, per_device(): lax.ppermute(here[:, :HALO], 'space', down).reshape(frames * span, depth)  4.89 us
  transfers between devices with their start and end apart: 16, of which 10 were waited for; matrix products, arithmetic and copies ran while one was open for 23% of the time, Pallas kernels for 5%

profile of v3, /device:TPU:0, one launch (start us, length us, event | category | flops | bytes accessed | tf_op | source)
XLA Modules:
  0.0 131.0 jit_solution(8240557996829528485)
XLA Ops:
  0.6 0.0 copy-start
  0.7 1.2 dynamic-slice_bitcast_fusion
  1.9 3.0 %collective-permute-start = (bf16[2,8,16,1024]{3,2,1,0:T(8,128)(2,1)S(1)}, bf16[2,8,16,1024]{3,2,1,0:T(8,128)(2,1)}, u32[]{:S(2)}, u32[]{:S(2)}) collective-permute-start(bf16[2,8,16,1024]{3,2,1,0:T(8,128)(2,1)S(1)} %dynamic-slice_bitcast_fusion), channel_id=1, source_target_pairs={{0,4},{4,0},{1,5},{5,1},{2,6},{6,2},{3,7},{7,3},{8,12},{12,8},{9,1... | collective-permute-start | bytes 1572872 | tf_op jit(solution)/shard_map/ppermute | solution.py:216
  4.9 1.3 %fusion.67 = (s32[1,1]{1,0:T(1,128)}, s32[1,1]{1,0:T(1,128)}) fusion(s32[1,2]{1,0:T(1,128)} %param.12), kind=kLoop, calls=%fused_computation.130 | loop fusion | bytes 16 | tf_op jit(solution)/shard_map/slice | solution.py:227
  6.3 0.8 fusion.63
  7.1 0.6 pad_add_fusion.k_order
  7.7 0.9 fusion.53.gather_ref
  8.6 0.8 fusion.54.spread_ref
  9.4 7.6 %collective-permute-done = bf16[2,8,16,1024]{3,2,1,0:T(8,128)(2,1)} collective-permute-done((bf16[2,8,16,1024]{3,2,1,0:T(8,128)(2,1)S(1)}, bf16[2,8,16,1024]{3,2,1,0:T(8,128)(2,1)}, u32[]{:S(2)}, u32[]{:S(2)}) %collective-permute-start) | collective-permute-done | bytes 524320 | tf_op jit(solution)/shard_map/ppermute | solution.py:216
  17.0 1.3 fusion.43
  18.2 0.1 pad_maximum_fusion
  18.4 0.3 multiply_reduce_fusion
  18.6 1.1 fusion.42
  19.7 1.1 fusion.66
  20.8 4.5 %collective-permute-start.1 = (bf16[2,4,32,1024]{3,2,1,0:T(8,128)(2,1)}, bf16[2,4,32,1024]{3,2,1,0:T(8,128)(2,1)}, u32[]{:S(2)}, u32[]{:S(2)}) collective-permute-start(bf16[2,4,32,1024]{3,2,1,0:T(8,128)(2,1)} %get-tuple-element.14), channel_id=1, source_target_pairs={{0,1},{1,2},{2,3},{4,5},{5,6},{6,7},{8,9},{9,10},{10,11},{12,13},{... | collective-permute-start | bytes 1572872 | tf_op jit(solution)/shard_map/ppermute | solution.py:220
  25.3 1.3 collective-permute-start.2
  26.6 0.1 rsqrt.52
  26.7 0.3 fusion.19
  27.0 7.7 %convolution_convert_fusion.q_ref.k_ref.v_ref = bf16[512,3072]{1,0:T(8,128)(2,1)} fusion(bf16[512,1024]{1,0:T(8,128)(2,1)S(1)} %fusion.19, bf16[1024,3072]{1,0:T(8,128)(2,1)} %param.14), kind=kOutput, calls=%fused_computation | convolution fusion | flops 3222798336 | bytes 10485760 | tf_op jit(solution)/shard_map/dot_general | solution.py:211
  34.8 0.4 collective-permute-done.1
  35.1 4.9 %collective-permute-done.2 = bf16[2,4,32,1024]{3,2,1,0:T(8,128)(2,1)} collective-permute-done((bf16[2,4,32,1024]{3,2,1,0:T(8,128)(2,1)}, bf16[2,4,32,1024]{3,2,1,0:T(8,128)(2,1)}, u32[]{:S(2)}, u32[]{:S(2)}) %collective-permute-start.2) | collective-permute-done | bytes 524320 | tf_op jit(solution)/shard_map/ppermute | solution.py:221
  40.0 1.5 %fusion.15 = f32[512]{0:T(512)S(1)} fusion(bf16[256,1024]{1,0:T(8,128)(2,1)} %bitcast.11, bf16[256,1024]{1,0:T(8,128)(2,1)} %bitcast.10), kind=kLoop, calls=%fused_computation.14 | loop fusion | flops 3145216 | bytes 1050624 | tf_op jit(solution)/shard_map/reduce_sum | solution.py:22
  41.5 5.0 %fusion.6.kt_ref.vt_ref.kb_ref.vb_ref = bf16[512,2048]{1,0:T(8,128)(2,1)} fusion(bf16[1024,3072]{1,0:T(8,128)(2,1)S(1)} %bitcast.56, f32[512]{0:T(512)S(1)} %add_rsqrt_fusion.1, f32[1024]{0:T(1024)S(1)} %copy-done.4, bf16[256,1024]{1,0:T(8,128)(2,1)} %bitcast.11, bf16[256,1024]{1,0:T(8,128)(2,1)} %bitcast.10), kind=kOutput, calls=%fused_computation.9 | convolution fusion | flops 2152202240 | bytes 7346176 | tf_op jit(solution)/shard_map/dot_general | solution.py:211
  46.6 7.1 %spatial.2 = bf16[256,1024]{1,0:T(8,128)(2,1)} custom-call(s32[1]{0:T(128)} %bitcast.6.reach_ref, s32[1]{0:T(128)} %bitcast.7.first_ref, bf16[512,3072]{1,0:T(8,128)(2,1)} %convolution_convert_fusion.q_ref.k_ref.v_ref, bf16[512,3072]{1,0:T(8,128)(2,1)} %convolution_convert_fusion.q_ref.k_ref.v_ref, ...), custom_call_target="tpu_custom_call" | custom-call | flops 9663676416 | bytes 3145728 | tf_op jit(solution)/shard_map/spatial/pallas_call | solution.py:79
  53.7 1.8 %fusion.20 = bf16[256,1024]{1,0:T(8,128)(2,1)S(1)} fusion(bf16[256,1024]{1,0:T(8,128)(2,1)} %spatial.2, bf16[1024,1024]{1,0:T(8,128)(2,1)S(1)} %copy-done, bf16[256,1024]{1,0:T(8,128)(2,1)S(1)} %bitcast.54), kind=kOutput, calls=%fused_computation.39 | convolution fusion | flops 537657344 | bytes 3670016 | tf_op jit(solution)/shard_map/dot_general | solution.py:232
  55.5 1.6 %collective-permute-start.3 = (bf16[256,1024]{1,0:T(8,128)(2,1)S(1)}, bf16[256,1024]{1,0:T(8,128)(2,1)S(1)}, u32[]{:S(2)}, u32[]{:S(2)}) collective-permute-start(bf16[256,1024]{1,0:T(8,128)(2,1)S(1)} %fusion.20), channel_id=1, source_target_pairs={{0,4},{4,0},{1,5},{5,1},{2,6},{6,2},{3,7},{7,3},{8,12},{12,8},{9,1... | collective-permute-start | bytes 1572872 | tf_op jit(solution)/shard_map/ppermute | solution.py:236
  57.0 0.2 fusion.22
  57.2 7.1 %spatial.3 = bf16[256,1024]{1,0:T(8,128)(2,1)} custom-call(s32[1]{0:T(128)} %bitcast.12.reach_ref, s32[1]{0:T(128)} %bitcast.7.first_ref, bf16[512,3072]{1,0:T(8,128)(2,1)} %convolution_convert_fusion.q_ref.k_ref.v_ref, bf16[512,3072]{1,0:T(8,128)(2,1)} %convolution_convert_fusion.q_ref.k_ref.v_ref, ...), custom_call_target="tpu_custom_call" | custom-call | flops 9663676416 | bytes 3145728 | tf_op jit(solution)/shard_map/spatial/pallas_call | solution.py:79
  64.3 2.2 %fusion.25 = (f32[256]{0:T(256)S(1)}, bf16[256,1024]{1,0:T(8,128)(2,1)S(1)}) fusion(bf16[256,1024]{1,0:T(8,128)(2,1)} %spatial.3, bf16[1024,1024]{1,0:T(8,128)(2,1)S(1)} %copy-done, bf16[256,1024]{1,0:T(8,128)(2,1)} %bitcast.53), kind=kOutput, calls=%fused_computation.44 | convolution fusion | flops 538443520 | bytes 3671040 | tf_op jit(solution)/shard_map/dot_general | solution.py:232
  66.5 0.6 collective-permute-start.4
  67.1 6.0 %convolution_convert_fusion.1.refs_1_.refs_3_.refs_7_ = bf16[256,3072]{1,0:T(8,128)(2,1)} fusion(bf16[1024,3072]{1,0:T(8,128)(2,1)} %param.17, bf16[256,1024]{1,0:T(8,128)(2,1)S(1)} %get-tuple-element.28, f32[256]{0:T(256)S(1)} %add_rsqrt_fusion.4, f32[1024]{0:T(1024)S(1)} %copy-done.8), kind=kOutput, calls=%fused_computation.3 | convolution fusion | flops 1612447744 | bytes 8393728 | tf_op jit(solution)/shard_map/dot_general | solution.py:211
  73.1 3.1 %convolution_convert_fusion.2.refs_0_.refs_2_.refs_6_ = bf16[256,3072]{1,0:T(8,128)(2,1)} fusion(bf16[1024,3072]{1,0:T(8,128)(2,1)S(1)} %bitcast.58, bf16[256,1024]{1,0:T(8,128)(2,1)S(1)} %fusion.20, f32[1024]{0:T(1024)S(1)} %copy-done.8, f32[256]{0:T(256)S(1)} %add_rsqrt_fusion.5), kind=kOutput, calls=%fused_computation.4 | convolution fusion | flops 1612447744 | bytes 8393728 | tf_op jit(solution)/shard_map/dot_general | solution.py:211
  76.2 2.3 %collective-permute-done.4 = bf16[256,1024]{1,0:T(8,128)(2,1)S(1)} collective-permute-done((bf16[256,1024]{1,0:T(8,128)(2,1)S(1)}, bf16[256,1024]{1,0:T(8,128)(2,1)S(1)}, u32[]{:S(2)}, u32[]{:S(2)}) %collective-permute-start.4) | collective-permute-done | bytes 524320 | tf_op jit(solution)/shard_map/ppermute | solution.py:236
  78.5 0.2 fusion.31
  78.7 0.2 fusion.28
  78.9 2.4 %fusion.12.refs_5_.refs_9_ = bf16[256,2048]{1,0:T(8,128)(2,1)} fusion(bf16[1024,3072]{1,0:T(8,128)(2,1)S(1)} %bitcast.58, bf16[256,1024]{1,0:T(8,128)(2,1)S(1)} %collective-permute-done.4, f32[256]{0:T(256)S(1)} %add_rsqrt_fusion.2, f32[1024]{0:T(1024)S(1)} %copy-done.8), kind=kOutput, calls=%fused_computation.13 | convolution fusion | flops 1075314688 | bytes 5772288 | tf_op jit(solution)/shard_map/dot_general | solution.py:211
  81.2 2.3 %fusion.9.refs_4_.refs_8_ = bf16[256,2048]{1,0:T(8,128)(2,1)} fusion(bf16[1024,3072]{1,0:T(8,128)(2,1)S(1)} %bitcast.58, bf16[256,1024]{1,0:T(8,128)(2,1)S(1)} %collective-permute-done.3, f32[256]{0:T(256)S(1)} %add_rsqrt_fusion.3, f32[1024]{0:T(1024)S(1)} %copy-done.8), kind=kOutput, calls=%fused_computation.12 | convolution fusion | flops 1075314688 | bytes 5772288 | tf_op jit(solution)/shard_map/dot_general | solution.py:211
  83.6 7.3 %temporal.1 = bf16[2,256,1024]{2,1,0:T(8,128)(2,1)} custom-call(s32[2]{0:T(128)} %copy-done.5, s32[4]{0:T(128)} %pad_add_fusion.k_order, bf16[1024,128]{1,0:T(8,128)(2,1)} %fusion.53.gather_ref, bf16[128,1024]{1,0:T(8,128)(2,1)} %fusion.54.spread_ref, bf16[256,3072]{1,0:T(8,128)(2,1)} %convolution_convert_fusion.2.refs_0_.refs_2_.refs_6_, ...), custom_call_target="tpu_custom_call" | custom-call | flops 1073741824 | bytes 4194304 | tf_op jit(solution)/shard_map/temporal/pallas_call | solution.py:124
  90.9 2.5 %convolution_convert_fusion.3 = bf16[1024,1024]{0,1:T(8,128)(2,1)S(1)} fusion(bf16[512,1024]{1,0:T(8,128)(2,1)} %bitcast.51, bf16[512,1024]{1,0:T(8,128)(2,1)S(1)} %bitcast.59), kind=kOutput, calls=%fused_computation.23 | convolution fusion | flops 1074790400 | bytes 4194304 | tf_op jit(solution)/shard_map/dot_general | solution.py:241
  93.4 1.3 %copy-done.1 = bf16[1024,1024]{0,1:T(8,128)(2,1)} copy-done((bf16[1024,1024]{0,1:T(8,128)(2,1)}, bf16[1024,1024]{0,1:T(8,128)(2,1)S(1)}, u32[]{:S(2)}) %copy-start.1) | copy-done | bytes 2097176
  94.7 0.1 constant_dynamic-slice_fusion.4
  94.8 0.1 collective-permute-start.5
  94.9 2.8 %collective-permute-done.5 = bf16[1024,512]{0,1:T(8,128)(2,1)} collective-permute-done((bf16[1024,512]{0,1:T(8,128)(2,1)S(1)}, bf16[1024,512]{0,1:T(8,128)(2,1)}, u32[]{:S(2)}, u32[]{:S(2)}) %collective-permute-start.5) | collective-permute-done | bytes 1048608 | tf_op jit(solution)/shard_map/ppermute | solution.py:145
  97.7 1.9 %add_convert_fusion = bf16[1024,512]{0,1:T(8,128)(2,1)S(1)} fusion(bf16[1024,512]{0,1:T(8,128)(2,1)} %collective-permute-done.5, bf16[1024,1024]{0,1:T(8,128)(2,1)} %copy-done.1, s32[]{:T(128)S(6)} %select_n.242), kind=kLoop, calls=%fused_computation.20 | loop fusion | flops 2097152 | bytes 3145732 | tf_op jit(solution)/shard_map/convert_element_type | solution.py:154
  99.6 0.1 fusion.65
  99.7 1.6 %collective-permute-start.8 = (bf16[512,256]{0,1:T(8,128)(2,1)S(1)}, bf16[512,256]{0,1:T(8,128)(2,1)}, u32[]{:S(2)}, u32[]{:S(2)}) collective-permute-start(bf16[512,256]{0,1:T(8,128)(2,1)S(1)} %constant_dynamic-slice_fusion.1), channel_id=1, source_target_pairs={{0,4},{4,0},{1,5},{5,1},{2,6},{6,2},{3,7},{7,3},{8,12},{12,8},{9,1... | collective-permute-start | bytes 786440 | tf_op jit(solution)/shard_map/ppermute | solution.py:163
  101.3 1.6 %collective-permute-start.6 = (bf16[1024,128]{0,1:T(8,128)(2,1)S(1)}, bf16[1024,128]{0,1:T(8,128)(2,1)S(1)}, u32[]{:S(2)}, u32[]{:S(2)}) collective-permute-start(bf16[1024,128]{0,1:T(8,128)(2,1)S(1)} %constant_dynamic-slice_fusion.3), channel_id=1, source_target_pairs={{0,16},{8,24},{16,0},{24,8},{1,17},{9,25},{17,1},{25,9},{2,18},{10... | collective-permute-start | bytes 786440 | tf_op jit(solution)/shard_map/ppermute | solution.py:145
  102.9 5.4 %collective-permute-done.8 = bf16[512,256]{0,1:T(8,128)(2,1)} collective-permute-done((bf16[512,256]{0,1:T(8,128)(2,1)S(1)}, bf16[512,256]{0,1:T(8,128)(2,1)}, u32[]{:S(2)}, u32[]{:S(2)}) %collective-permute-start.8) | collective-permute-done | bytes 262176 | tf_op jit(solution)/shard_map/ppermute | solution.py:163
  108.2 1.0 add_convert_fusion.2
  109.3 1.6 %collective-permute-start.9 = (bf16[512,128]{0,1:T(8,128)(2,1)S(1)}, bf16[512,128]{0,1:T(8,128)(2,1)S(1)}, u32[]{:S(2)}, u32[]{:S(2)}) collective-permute-start(bf16[512,128]{0,1:T(8,128)(2,1)S(1)} %constant_dynamic-slice_fusion), channel_id=1, source_target_pairs={{0,16},{8,24},{16,0},{24,8},{1,17},{9,25},{17,1},{25,9},{2,18},{10... | collective-permute-start | bytes 393224 | tf_op jit(solution)/shard_map/ppermute | solution.py:145
  110.9 0.1 add_convert_fusion.3
  111.0 1.5 %collective-permute-start.7 = (bf16[512,128]{0,1:T(8,128)(2,1)S(1)}, bf16[512,128]{0,1:T(8,128)(2,1)S(1)}, u32[]{:S(2)}, u32[]{:S(2)}) collective-permute-start(bf16[512,128]{0,1:T(8,128)(2,1)S(1)} %constant_dynamic-slice_fusion.2), channel_id=1, source_target_pairs={{0,4},{4,0},{1,5},{5,1},{2,6},{6,2},{3,7},{7,3},{8,12},{12,8},{9,1... | collective-permute-start | bytes 393224 | tf_op jit(solution)/shard_map/ppermute | solution.py:163
  112.5 1.8 %collective-permute-done.9 = bf16[512,128]{0,1:T(8,128)(2,1)S(1)} collective-permute-done((bf16[512,128]{0,1:T(8,128)(2,1)S(1)}, bf16[512,128]{0,1:T(8,128)(2,1)S(1)}, u32[]{:S(2)}, u32[]{:S(2)}) %collective-permute-start.9) | collective-permute-done | bytes 131104 | tf_op jit(solution)/shard_map/ppermute | solution.py:145
  114.4 1.7 %collective-permute-done.7 = bf16[512,128]{0,1:T(8,128)(2,1)S(1)} collective-permute-done((bf16[512,128]{0,1:T(8,128)(2,1)S(1)}, bf16[512,128]{0,1:T(8,128)(2,1)S(1)}, u32[]{:S(2)}, u32[]{:S(2)}) %collective-permute-start.7) | collective-permute-done | bytes 131104 | tf_op jit(solution)/shard_map/ppermute | solution.py:163
  116.1 0.9 collective-permute-start.10
  117.0 1.1 collective-permute-start.11
  118.1 2.8 %collective-permute-start.12 = (bf16[128,256]{0,1:T(8,128)(2,1)S(1)}, bf16[128,256]{0,1:T(8,128)(2,1)S(1)}, u32[]{:S(2)}, u32[]{:S(2)}) collective-permute-start(bf16[128,256]{0,1:T(8,128)(2,1)S(1)} %get-tuple-element.22), channel_id=1, source_target_pairs={{0,3},{1,0},{2,1},{3,2},{4,7},{5,4},{6,5},{7,6},{8,11},{9,8},{10,9... | collective-permute-start | bytes 196616 | tf_op jit(solution)/shard_map/ppermute | solution.py:163
  120.9 1.5 %collective-permute-done.10 = bf16[128,256]{0,1:T(8,128)(2,1)S(1)} collective-permute-done((bf16[128,256]{0,1:T(8,128)(2,1)S(1)}, bf16[128,256]{0,1:T(8,128)(2,1)S(1)}, u32[]{:S(2)}, u32[]{:S(2)}) %collective-permute-start.10) | collective-permute-done | bytes 65568 | tf_op jit(solution)/shard_map/ppermute | solution.py:163
  122.4 1.2 collective-permute-done.11
  123.6 0.1 collective-permute-start.13
  123.7 0.5 collective-permute-start.14
  124.2 1.3 collective-permute-start.15
  125.5 4.4 %add_convert_fusion.1 = bf16[512,1024]{1,0:T(8,128)(2,1)} fusion(bf16[512,1024]{1,0:T(8,128)(2,1)} %bitcast.52, bf16[1024,1024]{1,0:T(8,128)(2,1)} %param.18, bf16[256,1024]{1,0:T(8,128)(2,1)} %copy-done.7, bf16[256,1024]{1,0:T(8,128)(2,1)} %copy-done.2), kind=kOutput, calls=%fused_computation.21 | convolution fusion | flops 1076887552 | bytes 5242880 | tf_op jit(solution)/shard_map/dot_general | solution.py:244
  130.1 0.9 copy.13
  (56 shorter events, 0.5 us)
Async XLA Ops:
  0.6 53.1 %copy-start = (bf16[1024,1024]{1,0:T(8,128)(2,1)S(1)}, bf16[1024,1024]{1,0:T(8,128)(2,1)}, u32[]{:S(2)}) copy-start(bf16[1024,1024]{1,0:T(8,128)(2,1)} %param.15) | copy-start | bytes 6291460
  1.9 15.1 %collective-permute-start = (bf16[2,8,16,1024]{3,2,1,0:T(8,128)(2,1)S(1)}, bf16[2,8,16,1024]{3,2,1,0:T(8,128)(2,1)}, u32[]{:S(2)}, u32[]{:S(2)}) collective-permute-start(bf16[2,8,16,1024]{3,2,1,0:T(8,128)(2,1)S(1)} %dynamic-slice_bitcast_fusion), channel_id=1, source_target_pairs={{0,4},{4,0},{1,5},{5,1},{2,6},{6,2},{3,7},{7,3},{8,12},{12,8},{9,1... | collective-permute-start | bytes 1572872 | tf_op jit(solution)/shard_map/ppermute | solution.py:216
  7.1 11.3 %copy-start.5 = (s32[2]{0:T(128)}, s32[2]{0:T(128)S(1)}, u32[]{:S(2)}) copy-start(s32[2]{0:T(128)S(1)} %get-tuple-element.26.q_order) | copy-start | bytes 28
  18.6 8.1 %copy-start.4 = (f32[1024]{0:T(1024)S(1)}, f32[1024]{0:T(1024)}, u32[]{:S(2)}) copy-start(f32[1024]{0:T(1024)} %param.13) | copy-start | bytes 12292
  20.8 14.4 %collective-permute-start.1 = (bf16[2,4,32,1024]{3,2,1,0:T(8,128)(2,1)}, bf16[2,4,32,1024]{3,2,1,0:T(8,128)(2,1)}, u32[]{:S(2)}, u32[]{:S(2)}) collective-permute-start(bf16[2,4,32,1024]{3,2,1,0:T(8,128)(2,1)} %get-tuple-element.14), channel_id=1, source_target_pairs={{0,1},{1,2},{2,3},{4,5},{5,6},{6,7},{8,9},{9,10},{10,11},{12,13},{... | collective-permute-start | bytes 1572872 | tf_op jit(solution)/shard_map/ppermute | solution.py:220
  25.3 14.7 %collective-permute-start.2 = (bf16[2,4,32,1024]{3,2,1,0:T(8,128)(2,1)}, bf16[2,4,32,1024]{3,2,1,0:T(8,128)(2,1)}, u32[]{:S(2)}, u32[]{:S(2)}) collective-permute-start(bf16[2,4,32,1024]{3,2,1,0:T(8,128)(2,1)} %get-tuple-element.15), channel_id=1, source_target_pairs={{1,0},{2,1},{3,2},{5,4},{6,5},{7,6},{9,8},{10,9},{11,10},{13,12},{... | collective-permute-start | bytes 1572872 | tf_op jit(solution)/shard_map/ppermute | solution.py:221
  26.7 14.8 %slice-start = ((s8[6291456]{0:T(1024)(128)(4,1)}), s8[4194304]{0:T(1024)(128)(4,1)S(1)}, s32[]{:S(2)}) async-start(s8[6291456]{0:T(1024)(128)(4,1)} %bitcast.55), calls=%async_computation | async-start | bytes 8388608
  27.0 14.5 %slice-start.1 = ((s8[6291456]{0:T(1024)(128)(4,1)}), s8[2097152]{0:T(1024)(128)(4,1)S(1)}, s32[]{:S(2)}) async-start(s8[6291456]{0:T(1024)(128)(4,1)} %bitcast.55), calls=%async_computation.1 | async-start | bytes 4194304
  46.6 7.1 %copy-start.3 = (bf16[1,8,2,16,1024]{4,3,2,1,0:T(8,128)(2,1)S(1)}, bf16[1,8,2,16,1024]{4,3,2,1,0:T(8,128)(2,1)}, u32[]{:S(2)}) copy-start(bf16[1,8,2,16,1024]{4,3,2,1,0:T(8,128)(2,1)} %get-tuple-element.13) | copy-start | bytes 1572868
  55.5 17.6 %copy-start.2 = (bf16[256,1024]{1,0:T(8,128)(2,1)}, bf16[256,1024]{1,0:T(8,128)(2,1)S(1)}, u32[]{:S(2)}) copy-start(bf16[256,1024]{1,0:T(8,128)(2,1)S(1)} %fusion.20) | copy-start | bytes 1572868
  55.5 23.2 %collective-permute-start.3 = (bf16[256,1024]{1,0:T(8,128)(2,1)S(1)}, bf16[256,1024]{1,0:T(8,128)(2,1)S(1)}, u32[]{:S(2)}, u32[]{:S(2)}) collective-permute-start(bf16[256,1024]{1,0:T(8,128)(2,1)S(1)} %fusion.20), channel_id=1, source_target_pairs={{0,4},{4,0},{1,5},{5,1},{2,6},{6,2},{3,7},{7,3},{8,12},{12,8},{9,1... | collective-permute-start | bytes 1572872 | tf_op jit(solution)/shard_map/ppermute | solution.py:236
  64.3 2.8 %copy-start.8 = (f32[1024]{0:T(1024)S(1)}, f32[1024]{0:T(1024)}, u32[]{:S(2)}) copy-start(f32[1024]{0:T(1024)} %param.16) | copy-start | bytes 12292
  64.3 8.8 %slice-start.2 = ((s8[6291456]{0:T(1024)(128)(4,1)}), s8[4194304]{0:T(1024)(128)(4,1)S(1)}, s32[]{:S(2)}) async-start(s8[6291456]{0:T(1024)(128)(4,1)} %bitcast.57), calls=%async_computation.2 | async-start | bytes 8388608
  66.5 6.6 %copy-start.7 = (bf16[256,1024]{1,0:T(8,128)(2,1)}, bf16[256,1024]{1,0:T(8,128)(2,1)S(1)}, u32[]{:S(2)}) copy-start(bf16[256,1024]{1,0:T(8,128)(2,1)S(1)} %get-tuple-element.28) | copy-start | bytes 1572868
  66.5 12.0 %collective-permute-start.4 = (bf16[256,1024]{1,0:T(8,128)(2,1)S(1)}, bf16[256,1024]{1,0:T(8,128)(2,1)S(1)}, u32[]{:S(2)}, u32[]{:S(2)}) collective-permute-start(bf16[256,1024]{1,0:T(8,128)(2,1)S(1)} %get-tuple-element.28), channel_id=1, source_target_pairs={{0,4},{4,0},{1,5},{5,1},{2,6},{6,2},{3,7},{7,3},{8,12},{12,8},{9,1... | collective-permute-start | bytes 1572872 | tf_op jit(solution)/shard_map/ppermute | solution.py:236
  67.1 6.0 %slice-start.3 = ((s8[6291456]{0:T(1024)(128)(4,1)}), s8[2097152]{0:T(1024)(128)(4,1)S(1)}, s32[]{:S(2)}) async-start(s8[6291456]{0:T(1024)(128)(4,1)} %bitcast.57), calls=%async_computation.3 | async-start | bytes 4194304
  83.5 7.3 %copy-start.6 = (bf16[1,2,8,32,1024]{4,3,2,1,0:T(8,128)(2,1)S(1)}, bf16[1,2,8,32,1024]{4,3,2,1,0:T(8,128)(2,1)}, u32[]{:S(2)}) copy-start(bf16[1,2,8,32,1024]{4,3,2,1,0:T(8,128)(2,1)} %param.19) | copy-start | bytes 3145732
  93.4 1.3 %copy-start.1 = (bf16[1024,1024]{0,1:T(8,128)(2,1)}, bf16[1024,1024]{0,1:T(8,128)(2,1)S(1)}, u32[]{:S(2)}) copy-start(bf16[1024,1024]{0,1:T(8,128)(2,1)S(1)} %convolution_convert_fusion.3) | copy-start | bytes 6291460
  94.8 2.9 %collective-permute-start.5 = (bf16[1024,512]{0,1:T(8,128)(2,1)S(1)}, bf16[1024,512]{0,1:T(8,128)(2,1)}, u32[]{:S(2)}, u32[]{:S(2)}) collective-permute-start(bf16[1024,512]{0,1:T(8,128)(2,1)S(1)} %constant_dynamic-slice_fusion.4), channel_id=1, source_target_pairs={{0,8},{8,0},{16,24},{24,16},{1,9},{9,1},{17,25},{25,17},{2,10},{10... | collective-permute-start | bytes 3145736 | tf_op jit(solution)/shard_map/ppermute | solution.py:145
  99.7 8.5 %collective-permute-start.8 = (bf16[512,256]{0,1:T(8,128)(2,1)S(1)}, bf16[512,256]{0,1:T(8,128)(2,1)}, u32[]{:S(2)}, u32[]{:S(2)}) collective-permute-start(bf16[512,256]{0,1:T(8,128)(2,1)S(1)} %constant_dynamic-slice_fusion.1), channel_id=1, source_target_pairs={{0,4},{4,0},{1,5},{5,1},{2,6},{6,2},{3,7},{7,3},{8,12},{12,8},{9,1... | collective-permute-start | bytes 786440 | tf_op jit(solution)/shard_map/ppermute | solution.py:163
  101.3 9.6 %collective-permute-start.6 = (bf16[1024,128]{0,1:T(8,128)(2,1)S(1)}, bf16[1024,128]{0,1:T(8,128)(2,1)S(1)}, u32[]{:S(2)}, u32[]{:S(2)}) collective-permute-start(bf16[1024,128]{0,1:T(8,128)(2,1)S(1)} %constant_dynamic-slice_fusion.3), channel_id=1, source_target_pairs={{0,16},{8,24},{16,0},{24,8},{1,17},{9,25},{17,1},{25,9},{2,18},{10... | collective-permute-start | bytes 786440 | tf_op jit(solution)/shard_map/ppermute | solution.py:145
  109.3 5.0 %collective-permute-start.9 = (bf16[512,128]{0,1:T(8,128)(2,1)S(1)}, bf16[512,128]{0,1:T(8,128)(2,1)S(1)}, u32[]{:S(2)}, u32[]{:S(2)}) collective-permute-start(bf16[512,128]{0,1:T(8,128)(2,1)S(1)} %constant_dynamic-slice_fusion), channel_id=1, source_target_pairs={{0,16},{8,24},{16,0},{24,8},{1,17},{9,25},{17,1},{25,9},{2,18},{10... | collective-permute-start | bytes 393224 | tf_op jit(solution)/shard_map/ppermute | solution.py:145
  111.0 5.0 %collective-permute-start.7 = (bf16[512,128]{0,1:T(8,128)(2,1)S(1)}, bf16[512,128]{0,1:T(8,128)(2,1)S(1)}, u32[]{:S(2)}, u32[]{:S(2)}) collective-permute-start(bf16[512,128]{0,1:T(8,128)(2,1)S(1)} %constant_dynamic-slice_fusion.2), channel_id=1, source_target_pairs={{0,4},{4,0},{1,5},{5,1},{2,6},{6,2},{3,7},{7,3},{8,12},{12,8},{9,1... | collective-permute-start | bytes 393224 | tf_op jit(solution)/shard_map/ppermute | solution.py:163
  116.1 6.2 %collective-permute-start.10 = (bf16[128,256]{0,1:T(8,128)(2,1)S(1)}, bf16[128,256]{0,1:T(8,128)(2,1)S(1)}, u32[]{:S(2)}, u32[]{:S(2)}) collective-permute-start(bf16[128,256]{0,1:T(8,128)(2,1)S(1)} %get-tuple-element.20), channel_id=1, source_target_pairs={{0,1},{1,2},{2,3},{3,0},{4,5},{5,6},{6,7},{7,4},{8,9},{9,10},{10,1... | collective-permute-start | bytes 196616 | tf_op jit(solution)/shard_map/ppermute | solution.py:163
  117.0 6.6 %collective-permute-start.11 = (bf16[128,256]{0,1:T(8,128)(2,1)S(1)}, bf16[128,256]{0,1:T(8,128)(2,1)S(1)}, u32[]{:S(2)}, u32[]{:S(2)}) collective-permute-start(bf16[128,256]{0,1:T(8,128)(2,1)S(1)} %get-tuple-element.21), channel_id=1, source_target_pairs={{0,2},{1,3},{2,0},{3,1},{4,6},{5,7},{6,4},{7,5},{8,10},{9,11},{10,... | collective-permute-start | bytes 196616 | tf_op jit(solution)/shard_map/ppermute | solution.py:163
  118.1 5.5 %collective-permute-start.12 = (bf16[128,256]{0,1:T(8,128)(2,1)S(1)}, bf16[128,256]{0,1:T(8,128)(2,1)S(1)}, u32[]{:S(2)}, u32[]{:S(2)}) collective-permute-start(bf16[128,256]{0,1:T(8,128)(2,1)S(1)} %get-tuple-element.22), channel_id=1, source_target_pairs={{0,3},{1,0},{2,1},{3,2},{4,7},{5,4},{6,5},{7,6},{8,11},{9,8},{10,9... | collective-permute-start | bytes 196616 | tf_op jit(solution)/shard_map/ppermute | solution.py:163
  123.6 6.3 %collective-permute-start.13 = (bf16[128,256]{0,1:T(8,128)(2,1)S(1)}, bf16[128,256]{0,1:T(8,128)(2,1)S(1)}, u32[]{:S(2)}, u32[]{:S(2)}) collective-permute-start(bf16[128,256]{0,1:T(8,128)(2,1)S(1)} %add_convert_fusion.6), channel_id=1, source_target_pairs={{0,8},{8,0},{16,24},{24,16},{1,9},{9,1},{17,25},{25,17},{2,10},{10... | collective-permute-start | bytes 196616 | tf_op jit(solution)/shard_map/ppermute | solution.py:145
  123.7 6.2 %collective-permute-start.14 = (bf16[128,256]{0,1:T(8,128)(2,1)S(1)}, bf16[128,256]{0,1:T(8,128)(2,1)S(1)}, u32[]{:S(2)}, u32[]{:S(2)}) collective-permute-start(bf16[128,256]{0,1:T(8,128)(2,1)S(1)} %add_convert_fusion.6), channel_id=1, source_target_pairs={{0,16},{8,24},{16,0},{24,8},{1,17},{9,25},{17,1},{25,9},{2,18},{10... | collective-permute-start | bytes 196616 | tf_op jit(solution)/shard_map/ppermute | solution.py:145
  124.2 5.7 %collective-permute-start.15 = (bf16[128,256]{0,1:T(8,128)(2,1)S(1)}, bf16[128,256]{0,1:T(8,128)(2,1)S(1)}, u32[]{:S(2)}, u32[]{:S(2)}) collective-permute-start(bf16[128,256]{0,1:T(8,128)(2,1)S(1)} %add_convert_fusion.6), channel_id=1, source_target_pairs={{0,24},{8,16},{16,8},{24,0},{1,25},{9,17},{17,9},{25,1},{2,26},{10... | collective-permute-start | bytes 196616 | tf_op jit(solution)/shard_map/ppermute | solution.py:145
